TPU v7x, 32 devices: a whole 2x2x4 slice. The times are simulated.
32 devices in a mesh: grp: 4 (over y, x), dom: 8 (over z, core).
Axes of the slice: x: 2, y: 2, z: 4, core: 2. Of those that a mesh axis runs over, the one named last changes fastest.
Arguments:
- fields: float32 [210, 32768], P(None, ('grp', 'dom')), may hold values from -6 to 6
- metric: float32 [9, 32768], P(None, ('grp', 'dom')), may hold values from -5 to 5
- normals: float32 [12, 32768], P(None, ('grp', 'dom')), may hold values from -3 to 3
- fscale: float32 [4, 32768], P(None, ('grp', 'dom')), may hold values from 0.5 to 4
- orders: int32 [32768], P(('grp', 'dom')), may hold values from 1 to 4, as said below
- slots: int32 [32768], P(('grp', 'dom')), may hold values from 0 to 511, as said below
- send_faces: int32 [294912], P(('grp', 'dom')), may hold values from 0 to 8192, as said below
- recv_faces: int32 [262144], P(('grp', 'dom')), may hold values from 0 to 9216, as said below
- dmat: float32 [4, 105, 35], P('grp'), may hold values from -4 to 4
- tmat: float32 [4, 60, 35], P('grp'), may hold values from -4 to 4
- lmat: float32 [4, 35, 60], P('grp'), may hold values from -3 to 3
Outputs:
- rhs: float32 [210, 65536], P(None, ('grp', 'dom'))
Inputs may be any that keep to these rules, and one draw needn't show every extreme that they name: `orders`: on each device every order from 1 to 4 is held by at least one element and by at most 512; one order is held by exactly 512. The elements of one device that share an order have distinct slots. `send_faces`: each entry names a face of an occupied slot of the sending bucket or equals 4 * 2048 (nothing); in each list the items in use stand first. `recv_faces`: every face of an occupied slot names a distinct received item that is in use, and every item in use is named by exactly one face; faces of empty slots hold 9216. A list carries at most 768 items in use, and some list carries exactly 768.
All inputs are finite; a program needn't handle non-finite values.
Results may differ from a plain program's by a relative error of at most 0.0003.
Values sent between devices are 32-bit elements; how exact they have to be, the bound alone decides.
A program may use at most 128 MiB of HBM per device.

v0:
```python
import functools

import jax
import jax.numpy as jnp
from jax import lax
from jax.experimental import pallas as pl
from jax.experimental.pallas import tpu as pltpu
from jax.sharding import PartitionSpec as P

NPM = 35
FPTS = 15
COMPS = 6
FACES = 4
PP = 16
DP = 40
LANES = 128
TR = COMPS * PP
GEO = COMPS * NPM
METRIC, NORMAL, SCALE = GEO, GEO + 9, GEO + 21
ROWS = GEO + 30
BIG = 3 * DP + FACES * PP
MESH = pl.DeviceIdType.MESH
VMEM_LIMIT = 32 * 1024 * 1024


def split(x):
    high = x.astype(jnp.bfloat16)
    low = (x - high.astype(jnp.float32)).astype(jnp.bfloat16)
    return high, low


def dot3(a, b, dims):
    ah, al = a
    bh, bl = b

    def mul(x, y):
        return lax.dot_general(x, y, (dims, ((), ())), preferred_element_type=jnp.float32)

    return mul(ah, bh) + (mul(ah, bl) + mul(al, bh))


def params(**kw):
    return pltpu.CompilerParams(vmem_limit_bytes=VMEM_LIMIT, **kw)


VM = pl.BlockSpec(memory_space=pltpu.VMEM)
SM = pl.BlockSpec(memory_space=pltpu.SMEM)


def partner(g, d, groups):
    if groups & (groups - 1):
        return lax.rem(g + d, groups)
    other = g
    bit = 1
    while bit <= d:
        if d & bit:
            other = other + bit - 2 * bit * lax.rem(g // bit, 2)
        bit *= 2
    return other


def source(g, d, groups):
    if groups & (groups - 1):
        return lax.rem(g - d + groups, groups)
    return partner(g, d, groups)


def bucket_kernel(
    groups, cap, target_ref, fields_ref, metric_ref, normals_ref, fscale_ref, out_ref, pay, sbuf, send_sem, recv_sem
):
    g = lax.axis_index("grp")
    p = lax.axis_index("dom")
    barrier = pltpu.get_barrier_semaphore()
    for d in range(1, groups):
        pl.semaphore_signal(barrier, inc=1, device_id=(partner(g, d, groups), p), device_id_type=MESH)
    pay[0:GEO, :] = fields_ref[...]
    pay[METRIC : METRIC + 9, :] = metric_ref[...]
    pay[NORMAL : NORMAL + 12, :] = normals_ref[...]
    pay[SCALE : SCALE + 4, :] = fscale_ref[...]
    pay[SCALE + 4 : ROWS, :] = jnp.zeros((ROWS - SCALE - 4, pay.shape[1]), jnp.float32)
    high, low = split(pay[...])
    elements = pay.shape[1]
    target = target_ref[...]
    step = min(cap, 256)
    dims = (((1,), (1,)), ((), ()))

    def build(h, dst):
        for k in range(0, cap, step):
            ids = lax.broadcasted_iota(jnp.int32, (step, elements), 0) + (h * cap + k)
            hot = jnp.where(ids == target, 1.0, 0.0).astype(jnp.bfloat16)
            dst[:, k : k + step] = lax.dot_general(
                high, hot, dims, preferred_element_type=jnp.float32
            ) + lax.dot_general(low, hot, dims, preferred_element_type=jnp.float32)

    copies = [
        pltpu.make_async_remote_copy(
            src_ref=sbuf.at[d - 1],
            dst_ref=out_ref.at[g],
            send_sem=send_sem.at[d - 1],
            recv_sem=recv_sem.at[d - 1],
            device_id=(partner(g, d, groups), p),
            device_id_type=MESH,
        )
        for d in range(1, groups)
    ]
    build(partner(g, 1, groups), sbuf.at[0])
    pl.semaphore_wait(barrier, groups - 1)
    for d in range(2, groups):
        build(partner(g, d, groups), sbuf.at[d - 1])
        copies[d - 2].start()
    build(g, out_ref.at[g])
    copies[groups - 2].start()
    for d in range(1, groups):
        src = source(g, d, groups)
        pltpu.make_async_remote_copy(
            src_ref=sbuf.at[d - 1],
            dst_ref=out_ref.at[src],
            send_sem=send_sem.at[d - 1],
            recv_sem=recv_sem.at[d - 1],
            device_id=(partner(g, d, groups), p),
            device_id_type=MESH,
        ).wait_recv()
    for copy in copies:
        copy.wait_send()


def gather_block(index_ref, base, table, tmp):
    for i in range(LANES):
        tmp[i : i + 1, :] = table[pl.ds(index_ref[base + i], 1), :]


def exchange_kernel(
    groups, doms, cap, list_size, send_ref, bucket_ref, tt_ref, out_ref, table, tmp, sbuf, arrived, send_sem, recv_sem
):
    g = lax.axis_index("grp")
    p = lax.axis_index("dom")
    slots = groups * cap
    blocks = list_size // LANES
    lists = 3 * groups
    plan = [(d, j) for j in (2, 0, 1) for d in (1, 2, 0) if (d, j) != (0, 1) and d < groups]
    plan += [(d, j) for d in range(3, groups) for j in (2, 0, 1)]
    barrier = pltpu.get_barrier_semaphore()

    def peer(d, j):
        return (partner(g, d, groups), lax.rem(p + j - 1 + doms, doms))

    for d, j in plan:
        pl.semaphore_signal(barrier, inc=1, device_id=peer(d, j), device_id_type=MESH)

    weights = split(tt_ref[...])
    for b in range(groups):
        coefs = split(bucket_ref[b])
        for f in range(FACES):
            w = tuple(x[f * LANES : (f + 1) * LANES, :] for x in weights)
            table[f * slots + b * cap : f * slots + (b + 1) * cap, :] = dot3(coefs, w, ((0,), (1,)))
    table[FACES * slots : FACES * slots + 8, :] = jnp.zeros((8, LANES), jnp.float32)
    pl.semaphore_wait(barrier, len(plan))

    copies = []
    for n, (d, j) in enumerate(plan):
        base = (j * groups + partner(g, d, groups)) * list_size

        def pair(i, _, n=n, base=base):
            for k in range(2):
                at = pl.multiple_of((2 * i + k) * LANES, LANES)
                gather_block(send_ref, base + at, table, tmp.at[k])
                sbuf[n, :, pl.ds(at, LANES)] = tmp[k].T[:TR]
            return 0

        lax.fori_loop(0, blocks // 2, pair, 0)
        copies.append(
            pltpu.make_async_remote_copy(
                src_ref=sbuf.at[n],
                dst_ref=arrived.at[n],
                send_sem=send_sem.at[n],
                recv_sem=recv_sem.at[n],
                device_id=peer(d, j),
                device_id_type=MESH,
            )
        )
        if n:
            copies[n - 1].start()

    own = (groups + g) * list_size

    def own_block(i, _):
        at = pl.multiple_of(own + i * LANES, LANES)
        gather_block(send_ref, at, table, tmp.at[0])
        out_ref[pl.ds(at, LANES), :] = tmp[0]
        return 0

    lax.fori_loop(0, blocks, own_block, 0)
    copies[-1].start()
    out_ref[lists * list_size : lists * list_size + 8, :] = jnp.zeros((8, LANES), jnp.float32)
    fill = jnp.zeros((LANES - TR, LANES), jnp.float32)
    for n, (d, j) in enumerate(plan):
        copies[n].wait_recv()
        base = (j * groups + source(g, d, groups)) * list_size
        for q in range(blocks):
            block = jnp.concatenate([arrived[n, :, q * LANES : (q + 1) * LANES], fill], 0)
            out_ref[pl.ds(pl.multiple_of(base + q * LANES, LANES), LANES), :] = block.T
    for copy in copies:
        copy.wait_send()


def cross_of(u, v):
    return [u[1] * v[2] - u[2] * v[1], u[2] * v[0] - u[0] * v[2], u[0] * v[1] - u[1] * v[0]]


CURL = ((5, 1, 4, 2), (3, 2, 5, 0), (4, 0, 3, 1), (1, 2, 2, 1), (2, 0, 0, 2), (0, 1, 1, 0))


def final_kernel(
    groups, cap, recv_ref, table, bucket_ref, tt_ref, big_ref, out_ref, tmp, far, flux, stack
):
    slots = groups * cap
    stack[...] = jnp.zeros_like(stack)
    weights = split(tt_ref[...])
    big = split(big_ref[...])

    for g in range(groups):

        def one_face(f, _):
            for q in range(cap // LANES):
                gather_block(recv_ref, f * slots + g * cap + q * LANES, table, tmp.at[q % 2])
                far[f, :, q * LANES : (q + 1) * LANES] = tmp[q % 2].T[:TR]
            return 0

        lax.fori_loop(0, FACES, one_face, 0)
        block = bucket_ref[g]
        pieces = split(block)
        for f in range(FACES):
            own = dot3(tuple(x[f * LANES : f * LANES + TR, :] for x in weights), pieces, ((1,), (0,)))
            jump = far[f] - own
            jumps = [jump[c * PP : (c + 1) * PP, :] for c in range(COMPS)]
            n = [block[NORMAL + c * FACES + f : NORMAL + c * FACES + f + 1, :] for c in range(3)]
            s = 0.5 * block[SCALE + f : SCALE + f + 1, :]
            je, jh = jumps[:3], jumps[3:]
            ne = n[0] * je[0] + n[1] * je[1] + n[2] * je[2]
            nh = n[0] * jh[0] + n[1] * jh[1] + n[2] * jh[2]
            th, te = cross_of(n, jh), cross_of(n, je)
            for c in range(3):
                flux[c, f * PP : (f + 1) * PP, :] = s * (th[c] + je[c] - n[c] * ne)
                flux[3 + c, f * PP : (f + 1) * PP, :] = s * (jh[c] - te[c] - n[c] * nh)
        coefs = [bucket_ref[g, c * NPM : (c + 1) * NPM, :] for c in range(COMPS)]
        for c in range(COMPS):
            q1, x1, q2, x2 = CURL[c]
            for a in range(3):
                m1 = block[METRIC + 3 * a + x1 : METRIC + 3 * a + x1 + 1, :]
                m2 = block[METRIC + 3 * a + x2 : METRIC + 3 * a + x2 + 1, :]
                stack[a * DP : a * DP + NPM, :] = m1 * coefs[q1] - m2 * coefs[q2]
            stack[3 * DP : BIG, :] = flux[c]
            result = dot3(big, split(stack[...]), ((1,), (0,)))
            out_ref[c * NPM : (c + 1) * NPM, g * cap : (g + 1) * cap] = result[:NPM]


def local(groups, doms, fields, metric, normals, fscale, orders, slots, send_faces, recv_faces, dmat, tmat, lmat):
    own_group = lax.axis_index("grp")
    elements = fields.shape[1]
    cap = elements // 2
    total = groups * cap
    lists = 3 * groups
    list_size = send_faces.shape[0] // lists
    f32 = jnp.float32
    target = ((orders - 1) * cap + slots).reshape(1, elements)
    bucket = pl.pallas_call(
        functools.partial(bucket_kernel, groups, cap),
        out_shape=jax.ShapeDtypeStruct((groups, ROWS, cap), f32),
        in_specs=[VM] * 5,
        out_specs=VM,
        scratch_shapes=[
            pltpu.VMEM((ROWS, elements), f32),
            pltpu.VMEM((groups - 1, ROWS, cap), f32),
            pltpu.SemaphoreType.DMA((groups - 1,)),
            pltpu.SemaphoreType.DMA((groups - 1,)),
        ],
        compiler_params=params(collective_id=1, has_side_effects=True),
        name="bucket",
    )(target, fields, metric, normals, fscale)

    node_total = (own_group + 2) * (own_group + 3) * (own_group + 4) // 6
    mask = (jnp.arange(NPM, dtype=jnp.int32) < node_total).astype(f32)
    deriv = dmat[0].reshape(3, NPM, NPM) * mask[None, :, None] * mask[None, None, :]
    deriv = jnp.pad(jnp.transpose(deriv, (1, 0, 2)), ((0, 0), (0, 0), (0, DP - NPM))).reshape(NPM, 3 * DP)
    lift = jnp.transpose((lmat[0] * mask[:, None]).reshape(NPM, FPTS, FACES), (0, 2, 1))
    lift = jnp.pad(lift, ((0, 0), (0, 0), (0, PP - FPTS))).reshape(NPM, FACES * PP)
    big = jnp.pad(jnp.concatenate([deriv, lift], 1), ((0, DP - NPM), (0, 0)))
    trace = jnp.transpose((tmat[0] * mask[None, :]).reshape(FPTS, FACES, NPM), (1, 0, 2))
    trace = jnp.pad(trace, ((0, 0), (0, PP - FPTS), (0, 0)))
    wide = [
        jnp.pad(trace, ((0, 0), (0, 0), (c * NPM, ROWS - (c + 1) * NPM))) for c in range(COMPS)
    ] + [jnp.zeros((FACES, LANES - TR, ROWS), f32)]
    tt = jnp.concatenate(wide, 1).reshape(FACES * LANES, ROWS)

    received = pl.pallas_call(
        functools.partial(exchange_kernel, groups, doms, cap, list_size),
        out_shape=jax.ShapeDtypeStruct((lists * list_size + 8, LANES), f32),
        in_specs=[SM, VM, VM],
        out_specs=VM,
        scratch_shapes=[
            pltpu.VMEM((FACES * total + 8, LANES), f32),
            pltpu.VMEM((2, LANES, LANES), f32),
            pltpu.VMEM((lists - 1, TR, list_size), f32),
            pltpu.VMEM((lists - 1, TR, list_size), f32),
            pltpu.SemaphoreType.DMA((lists - 1,)),
            pltpu.SemaphoreType.DMA((lists - 1,)),
        ],
        compiler_params=params(collective_id=0, has_side_effects=True),
        name="exchange",
    )(send_faces, bucket, tt)
    return pl.pallas_call(
        functools.partial(final_kernel, groups, cap),
        out_shape=jax.ShapeDtypeStruct((GEO, total), f32),
        in_specs=[SM, VM, VM, VM, VM],
        out_specs=VM,
        scratch_shapes=[
            pltpu.VMEM((2, LANES, LANES), f32),
            pltpu.VMEM((FACES, TR, cap), f32),
            pltpu.VMEM((COMPS, FACES * PP, cap), f32),
            pltpu.VMEM((BIG, cap), f32),
        ],
        compiler_params=params(),
        name="final",
    )(recv_faces, received, bucket, tt, big)


def solution(mesh):
    col = P(None, ("grp", "dom"))
    row = P(("grp", "dom"))
    mat = P("grp", None, None)
    in_specs = (col, col, col, col, row, row, row, row, mat, mat, mat)
    body = functools.partial(local, mesh.shape["grp"], mesh.shape["dom"])
    return jax.shard_map(body, mesh=mesh, in_specs=in_specs, out_specs=col, check_vma=False)
```

profile of v0, /device:TPU:0, one launch (start us, length us, event | category | flops | bytes accessed | tf_op | source)
XLA Modules:
  0.0 98.0 jit_solution(1393509755707222629)
XLA Ops:
  0.0 0.0 copy-start.5
  0.0 0.0 copy-start.2
  0.0 0.0 copy-start.1
  0.0 0.0 copy-start
  0.0 0.8 multiply_add_fusion
  0.8 0.8 reduce
  1.6 0.8 copy.15
  2.5 0.8 copy.23
  3.3 0.1 copy.25
  3.4 0.1 reshape_squeeze.3
  3.5 0.1 multiply_bitcast_fusion
  3.6 0.1 copy.32
  3.8 0.0 copy-start.3
  3.8 0.1 reshape.48
  3.9 0.1 select_maximum_fusion.big_ref
  4.0 0.1 pad_dynamic-update-slice_fusion.4
  4.1 0.1 pad_dynamic-update-slice_fusion.3
  4.2 0.1 pad_dynamic-update-slice_fusion.2
  4.2 0.1 pad_dynamic-update-slice_fusion.1
  4.3 0.1 pad_dynamic-update-slice_fusion
  4.4 0.0 copy-done.5
  4.4 0.0 copy-done.2
  4.4 0.0 copy-done.1
  4.5 0.0 copy-done
  4.5 27.7 %bucket.1.bucket_ref = f32[4,240,512]{2,1,0:T(8,128)S(1)} custom-call(s32[1,1024]{1,0:T(1,128)S(1)} %bitcast.15, f32[210,1024]{1,0:T(8,128)S(1)} %copy-done, f32[9,1024]{1,0:T(8,128)S(1)} %copy-done.1, f32[12,1024]{1,0:T(8,128)S(1)} %copy-done.2, f32[4,1024]{1,0:T(4,128)S(1)} %copy-done.5), custom_call_target="tpu_custom_call" | custom-call | tf_op jit(solution)/shard_map/bucket/pallas_call | solution.py:266
  32.2 0.0 copy-done.3
  32.2 0.0 copy-start.4
  32.2 47.4 %exchange.1.table = f32[9224,128]{1,0:T(8,128)S(1)} custom-call(s32[9216]{0:T(1024)S(1)} %copy-done.3, f32[4,240,512]{2,1,0:T(8,128)S(1)} %bucket.1.bucket_ref, f32[512,240]{1,0:T(8,128)S(1)} %bitcast.13), custom_call_target="tpu_custom_call" | custom-call | tf_op jit(solution)/shard_map/exchange/pallas_call | solution.py:295
  79.7 0.0 copy-done.4
  79.7 18.3 %final.1 = f32[210,2048]{1,0:T(8,128)} custom-call(s32[8192]{0:T(1024)S(1)} %copy-done.4, f32[9224,128]{1,0:T(8,128)S(1)} %exchange.1.table, f32[4,240,512]{2,1,0:T(8,128)S(1)} %bucket.1.bucket_ref, f32[512,240]{1,0:T(8,128)S(1)} %bitcast.14, f32[40,184]{1,0:T(8,128)S(1)} %select_maximum_fusion.big_ref), custom_call_target="tpu_custom_call" | custom-call | tf_op jit(solution)/shard_map/final/pallas_call | solution.py:311
  (12 shorter events, 0.1 us)
Async XLA Ops:
  0.0 4.4 %copy-start.5 = (f32[4,1024]{1,0:T(4,128)S(1)}, f32[4,1024]{1,0:T(4,128)}, u32[]{:S(2)}) copy-start(f32[4,1024]{1,0:T(4,128)} %fscale_ref.1) | copy-start | bytes 49156
  0.0 4.4 %copy-start.2 = (f32[12,1024]{1,0:T(8,128)S(1)}, f32[12,1024]{1,0:T(8,128)}, u32[]{:S(2)}) copy-start(f32[12,1024]{1,0:T(8,128)} %normals_ref.1) | copy-start | bytes 147460
  0.0 4.4 %copy-start.1 = (f32[9,1024]{1,0:T(8,128)S(1)}, f32[9,1024]{1,0:T(8,128)}, u32[]{:S(2)}) copy-start(f32[9,1024]{1,0:T(8,128)} %metric_ref.1) | copy-start | bytes 110596
  0.0 4.5 %copy-start = (f32[210,1024]{1,0:T(8,128)S(1)}, f32[210,1024]{1,0:T(8,128)}, u32[]{:S(2)}) copy-start(f32[210,1024]{1,0:T(8,128)} %fields_ref.1) | copy-start | bytes 2580484
  3.8 28.4 %copy-start.3 = (s32[9216]{0:T(1024)S(1)}, s32[9216]{0:T(1024)}, u32[]{:S(2)}) copy-start(s32[9216]{0:T(1024)} %send_ref.1) | copy-start | bytes 110596
  32.2 47.4 %copy-start.4 = (s32[8192]{0:T(1024)S(1)}, s32[8192]{0:T(1024)}, u32[]{:S(2)}) copy-start(s32[8192]{0:T(1024)} %recv_ref.1) | copy-start | bytes 98308
where the time goes:
time: 99.8 us; the launch traced here: 98 us
  Pallas kernels  93.5 us (94%)
  local copies, waits for them, and re-layouts  2.56 us (3%)
  other arithmetic  1.77 us (2%)
    pallas_call x1, Pallas kernels, local(): pl.pallas_call(functools.partial(exchange_kernel, groups, doms, cap, list...  47.4 us
    pallas_call x1, Pallas kernels, local(): pl.pallas_call(functools.partial(bucket_kernel, groups, cap), out_shape=j...  27.7 us
    pallas_call x1, Pallas kernels, local(): pl.pallas_call(functools.partial(final_kernel, groups, cap), out_shape=ja...  18.3 us
    unnamed x23, local copies, waits for them, and re-layouts  2.21 us

commit v1 on v0

v1 whole, which is shorter than its diff:
```python
import functools

import jax
import jax.numpy as jnp
from jax import lax
from jax.experimental import pallas as pl
from jax.experimental.pallas import tpu as pltpu
from jax.sharding import PartitionSpec as P

NPM = 35
FPTS = 15
COMPS = 6
FACES = 4
PP = 16
DP = 40
LANES = 128
TR = COMPS * PP
NODES = (4, 10, 20, 35)
STARTS = (0, 4, 10, 20)
N1 = NODES[0]
LOW = COMPS * N1
CODED = 32
METRIC, NORMAL, SCALE, ONE, GEO = 0, 9, 21, 25, 26
GROWS = 32
ROWS = 240
SENT = tuple(-(-(GEO + COMPS * n) // 8) * 8 for n in NODES)
BASES = tuple(GEO + COMPS * s for s in STARTS)
RELAYED = (2, 0)
MESH = pl.DeviceIdType.MESH
F32 = jnp.float32
BF16 = jnp.bfloat16
EXACT = lax.Precision.HIGHEST


def split(x):
    high = x.astype(BF16)
    low = (x - high.astype(F32)).astype(BF16)
    return high, low


def dot3(a, b, dims):
    ah, al = a
    bh, bl = b

    def mul(x, y):
        return lax.dot_general(x, y, (dims, ((), ())), preferred_element_type=F32)

    return mul(ah, bh) + (mul(ah, bl) + mul(al, bh))


def exact_dot(a, b, dims=((1,), (0,))):
    return lax.dot_general(a, b, (dims, ((), ())), precision=EXACT, preferred_element_type=F32)


def iotas(shape):
    return lax.broadcasted_iota(jnp.int32, shape, 0), lax.broadcasted_iota(jnp.int32, shape, 1)


def ones_where(cond):
    return jnp.where(cond, 1.0, 0.0).astype(F32)


VM = pl.BlockSpec(memory_space=pltpu.VMEM)
SM = pl.BlockSpec(memory_space=pltpu.SMEM)


def gather_block(index_ref, base, table, tmp):
    for i in range(LANES):
        tmp[i : i + 1, :] = table[pl.ds(index_ref[base + i], 1), :]


def flat_row(block):
    return jnp.concatenate([block[i : i + 1, :] for i in range(block.shape[0])], axis=1)


CURL = ((5, 1, 4, 2), (3, 2, 5, 0), (4, 0, 3, 1), (1, 2, 2, 1), (2, 0, 0, 2), (0, 1, 1, 0))


def place(c, shape):
    i, r = iotas(shape)
    target = BASES[3] + c * (NODES[3] - STARTS[3]) + (i - STARTS[3])
    for b in (2, 1, 0):
        width = NODES[b] - STARTS[b]
        target = jnp.where(i < NODES[b], BASES[b] + c * width + (i - STARTS[b]), target)
    return i, r, target


def move_kernel(
    groups, doms, cap, list_size,
    send_ref, orders_ref, slots_ref, fields_ref, metric_ref, normals_ref, fscale_ref, recv_ref, dmat_ref, tmat_ref, lmat_ref,
    far_ref, own_ref, vol_ref, geo_ref, lift_ref,
    pay, bsend, bucket, table, low_table, tmp, sbuf, arrived, relay, wide, wcat_h, wcat_l, tr_h, tr_l, dx_h, dx_l,
    derivs, l1x, t1x, faces_out, faces_in,
    bsend_sem, brecv_sem, ssem, rsem, relay_send, relay_recv, l1_send, l1_recv, t1_send, t1_recv, fsend_sem, frecv_sem,
):
    g = lax.axis_index("grp")
    p = lax.axis_index("dom")
    slots = groups * cap
    blocks = list_size // LANES
    elements = 2 * cap
    barrier = pltpu.get_barrier_semaphore()

    def dom_of(j):
        return lax.rem(p + j - 1 + doms, doms)

    for b in range(groups):
        bucket[b, SENT[0] : ROWS, :] = jnp.zeros((ROWS - SENT[0], cap), F32)
    for j in (1, 2, 0):
        for d in range(groups):
            if (j, d) != (1, 0):
                pl.semaphore_signal(
                    barrier, inc=1, device_id=(lax.rem(g + d, groups), dom_of(j)), device_id_type=MESH
                )

    pay[METRIC : METRIC + 9, :] = metric_ref[...]
    pay[NORMAL : NORMAL + 12, :] = normals_ref[...]
    pay[SCALE : SCALE + 4, :] = fscale_ref[...]
    pay[ONE : ONE + 1, :] = jnp.ones((1, elements), F32)
    for b in range(4):
        width = NODES[b] - STARTS[b]
        for c in range(COMPS):
            at = BASES[b] + c * width
            pay[at : at + width, :] = fields_ref[c * NPM + STARTS[b] : c * NPM + NODES[b], :]
    pay[GEO + COMPS * NPM : ROWS, :] = jnp.zeros((ROWS - GEO - COMPS * NPM, elements), F32)
    target = flat_row((orders_ref[...] - 1) * cap + slots_ref[...])
    high, low = split(pay[...])
    both = jnp.concatenate([high, low], axis=0)
    step = min(cap, 256)

    def build(h, dst):
        for k in range(0, cap, step):
            ids = lax.broadcasted_iota(jnp.int32, (step, elements), 0) + (h * cap + k)
            hot = jnp.where(ids == target, 1.0, 0.0).astype(BF16)
            out = lax.dot_general(both, hot, (((1,), (1,)), ((), ())), preferred_element_type=F32)
            dst[:, k : k + step] = out[:ROWS] + out[ROWS:]

    def goal(i):
        top = groups - 1 - i
        return top - jnp.where(top <= g, 1, 0)

    def bucket_copy(i, rows):
        return pltpu.make_async_remote_copy(
            src_ref=bsend.at[i, pl.ds(0, rows)],
            dst_ref=bucket.at[g, pl.ds(0, rows)],
            send_sem=bsend_sem.at[i],
            recv_sem=brecv_sem.at[g],
            device_id=(goal(i), p),
            device_id_type=MESH,
        )

    def for_goal(i, act):
        for h in (groups - 1 - i, groups - 2 - i):
            @pl.when(goal(i) == h)
            def _(h=h):
                act(bucket_copy(i, SENT[h]))

    build(goal(0), bsend.at[0])
    pl.semaphore_wait(barrier, 3 * groups - 1)
    for i in range(1, groups - 1):
        build(goal(i), bsend.at[i])
        for_goal(i - 1, lambda copy: copy.start())
    build(g, bucket.at[g])
    for_goal(groups - 2, lambda copy: copy.start())

    own_nodes = (g + 2) * (g + 3) * (g + 4) // 6
    wide[...] = jnp.zeros_like(wide)
    wide[0, 0 : FPTS * FACES, 0:NPM] = tmat_ref[...]
    wide[1, 0:NPM, 0 : FPTS * FACES] = lmat_ref[...]
    for a in range(3):
        wide[2 + a, 0:NPM, 0:NPM] = dmat_ref[a * NPM : (a + 1) * NPM, :]
    i, r = iotas((FACES * PP, LANES))
    order_points = ones_where((r == (i & (PP - 1)) * FACES + (i // PP)) & ((i & (PP - 1)) < FPTS))
    trace = exact_dot(order_points, wide[0])
    lift = exact_dot(wide[1, 0:DP], order_points, ((1,), (1,)))
    row = lax.broadcasted_iota(jnp.int32, (DP, FACES * PP), 0)
    lift = jnp.where(row < own_nodes, lift, 0.0)
    tr_f = [[] for _ in range(FACES)]
    node = lax.broadcasted_iota(jnp.int32, (DP, ROWS), 0)
    for c in range(COMPS):
        i, r, at = place(c, (LANES, ROWS))
        spread = ones_where((r == at) & (i < own_nodes) & (i < NPM))
        part = exact_dot(trace, spread)
        for f in range(FACES):
            tr_f[f].append(part[f * PP : (f + 1) * PP])
        for a in range(3):
            block = exact_dot(wide[2 + a, 0:DP], spread)
            block = split(jnp.where(node < own_nodes, block, 0.0))
            at_row = (a * COMPS + c) * DP
            dx_h[at_row : at_row + DP, :] = block[0]
            dx_l[at_row : at_row + DP, :] = block[1]
    tr_f = [jnp.concatenate(parts + [jnp.zeros((LANES - TR, ROWS), F32)], 0) for parts in tr_f]

    def fan(f):
        i, r = iotas((FACES * PP, LANES))
        return ones_where(i == f * PP + (r & (PP - 1)))

    def weight_copy(kind, h):
        src, send, recv = ((l1x, l1_send, l1_recv), (t1x, t1_send, t1_recv))[kind]
        return pltpu.make_async_remote_copy(
            src_ref=src, dst_ref=src, send_sem=send.at[h], recv_sem=recv.at[0],
            device_id=(h, p), device_id_type=MESH,
        )

    def face_copy(s, j):
        return pltpu.make_async_remote_copy(
            src_ref=faces_out.at[j * groups + s],
            dst_ref=faces_in.at[j],
            send_sem=fsend_sem.at[j * groups + s],
            recv_sem=frecv_sem.at[j],
            device_id=(s, lax.rem(p - j + 1 + doms, doms)),
            device_id_type=MESH,
        )

    def face_local():
        return pltpu.make_async_copy(faces_out.at[groups], faces_in.at[1], frecv_sem.at[1])

    @pl.when(g == 0)
    def _():
        i, r = iotas((LOW, DP))
        picked = exact_dot(ones_where(r == (i & (N1 - 1))), lift)
        i, r = iotas((CODED, LANES))
        picked_t = exact_dot(ones_where((r == (i & (N1 - 1))) & (i < LOW)), trace, ((1,), (1,)))
        for f in range(FACES):
            i, r = iotas((LOW, LANES))
            l1x[f * LOW : (f + 1) * LOW, :] = jnp.where((r // PP) == (i // N1), exact_dot(picked, fan(f)), 0.0)
            i, r = iotas((CODED, LANES))
            t1x[:, f * LANES : (f + 1) * LANES] = jnp.where(
                (r // PP) == (i // N1), exact_dot(picked_t, fan(f)), 0.0
            )
        rows = slots // LANES
        count = -(-(3 * groups * blocks) // 8) * 8
        found = jnp.zeros((count, LANES), F32)
        for f in range(1, FACES):
            entry = flat_row(recv_ref[f * rows : (f + 1) * rows, :])
            upper, lower = entry // LANES, entry & (LANES - 1)
            a = jnp.where(lax.broadcasted_iota(jnp.int32, (count, slots), 0) == upper, float(f), 0.0).astype(BF16)
            b = jnp.where(lax.broadcasted_iota(jnp.int32, (LANES, slots), 0) == lower, 1.0, 0.0).astype(BF16)
            found = found + lax.dot_general(a, b, (((1,), (1,)), ((), ())), preferred_element_type=F32)
        for n in range(3 * groups):
            faces_out[n, 0:blocks, :] = found[n * blocks : (n + 1) * blocks]
        for kind in range(2):
            for h in range(1, groups):
                weight_copy(kind, h).start()
        for s in range(groups):
            for j in range(3):
                (face_local() if (s, j) == (0, 1) else face_copy(s, j)).start()

    @pl.when(g != 0)
    def _():
        weight_copy(0, 1).wait_recv()

    for f in range(FACES):
        at = f * 2 * LANES
        for k, piece in enumerate(split(tr_f[f])):
            (tr_h, tr_l)[k][f * TR : (f + 1) * TR, :] = piece[:TR]
            (wcat_h, wcat_l)[k][at : at + LANES, :] = piece
        lowered = exact_dot(l1x[...], tr_f[f])
        filled = jnp.concatenate([lowered, jnp.zeros((LANES - TR, ROWS), F32)], 0)
        for k, piece in enumerate(split(filled)):
            (wcat_h, wcat_l)[k][at + LANES : at + 2 * LANES, :] = piece

        @pl.when(g == 0)
        def _(f=f, at=at, lowered=lowered):
            i, r = iotas((LANES, ROWS))
            coded = jnp.where((i < LOW) & (r == GEO + i), 1.0, 0.0) + jnp.where((i == LOW) & (r == ONE), float(f), 0.0)
            wcat_h[at : at + LANES, :] = coded.astype(BF16)
            wcat_l[at : at + LANES, :] = jnp.zeros((LANES, ROWS), BF16)
            i, r = iotas((TR, TR))
            pick = ones_where(((i & (PP - 1)) < N1) & (r == f * LOW + (i // PP) * N1 + (i & (PP - 1))))
            for k, piece in enumerate(split(exact_dot(pick, lowered))):
                (tr_h, tr_l)[k][f * TR : (f + 1) * TR, :] = piece

    i, r = iotas((DP, FACES * PP))
    unit = ones_where((i < N1) & ((r & (PP - 1)) == i))
    lift_ref[...] = jnp.where(g == 0, unit, lift)

    for t in (table, low_table):
        t[FACES * slots : FACES * slots + 8, :] = jnp.zeros((8, LANES), F32)

    def make_tables(b):
        coefs = split(bucket[b].T)
        for f in range(FACES):
            w = tuple(x[f * 2 * LANES : (f + 1) * 2 * LANES, :] for x in (wcat_h, wcat_l))
            rows = dot3(coefs, w, ((1,), (1,)))
            at = pl.multiple_of(f * slots + b * cap, LANES)
            table[pl.ds(at, cap), :] = rows[:, :LANES]
            low_table[pl.ds(at, cap), :] = rows[:, LANES:]

    def arrive(b):
        for h in range(groups):
            @pl.when(g == h)
            def _(h=h):
                pltpu.make_async_remote_copy(
                    src_ref=bsend.at[0, pl.ds(0, SENT[h])],
                    dst_ref=bucket.at[b, pl.ds(0, SENT[h])],
                    send_sem=bsend_sem.at[0],
                    recv_sem=brecv_sem.at[b],
                    device_id=(b, p),
                    device_id_type=MESH,
                ).wait_recv()

    def table_step(k, _):
        b = lax.rem(g + k, groups)

        @pl.when(k > 0)
        def _():
            arrive(b)

        make_tables(b)
        return 0

    lax.fori_loop(0, groups, table_step, 0)

    def list_copy(j, h, rows, dev=None, dst=None, recv=None):
        n = j * groups + h
        return pltpu.make_async_remote_copy(
            src_ref=sbuf.at[n, pl.ds(0, rows)],
            dst_ref=(arrived.at[j * groups + g] if dst is None else dst).at[pl.ds(0, rows)],
            send_sem=ssem.at[n],
            recv_sem=rsem.at[j * groups + g] if recv is None else recv,
            device_id=(h, dom_of(j)) if dev is None else dev,
            device_id_type=MESH,
        )

    def local_copy(h, rows):
        n = groups + h
        return pltpu.make_async_copy(sbuf.at[n, pl.ds(0, rows)], arrived.at[n, pl.ds(0, rows)], rsem.at[n])

    def relay_in(j):
        k = RELAYED.index(j)
        return list_copy(j, 1, TR, dev=(0, dom_of(j)), dst=relay.at[k], recv=relay_recv.at[k])

    def relay_out(j):
        k = RELAYED.index(j)
        return pltpu.make_async_remote_copy(
            src_ref=relay.at[k], dst_ref=arrived.at[j * groups + 2], send_sem=relay_send.at[k],
            recv_sem=rsem.at[j * groups + 2], device_id=(1, p), device_id_type=MESH,
        )

    def for_send(j, h, act, act_local):
        if h == 0:
            if j != 1:
                act(list_copy(j, h, LOW))
            else:
                @pl.when(g != 0)
                def _():
                    act(list_copy(j, h, LOW))

                @pl.when(g == 0)
                def _():
                    act_local(local_copy(h, LOW))
            return

        @pl.when(g == 0)
        def _():
            act(list_copy(j, h, CODED))

        plain = g != 0
        if j == 1:
            plain = jnp.logical_and(plain, g != h)

            @pl.when(g == h)
            def _():
                act_local(local_copy(h, TR))
        if h == 1 and j in RELAYED:
            plain = jnp.logical_and(plain, g != 2)

            @pl.when(g == 2)
            def _():
                act(relay_in(j))

        @pl.when(plain)
        def _():
            act(list_copy(j, h, TR))

    order = [(j, h) for j in (2, 0, 1) for h in (1, 3, 2)] + [(j, 0) for j in (2, 0, 1)]
    before = None
    for j, h in order:
        n = j * groups + h
        if h == 0:
            @pl.when(jnp.logical_or(g != 0, j != 1))
            def _(j=j):
                pltpu.make_async_remote_copy(
                    src_ref=faces_out.at[0], dst_ref=faces_in.at[j], send_sem=fsend_sem.at[0],
                    recv_sem=frecv_sem.at[j], device_id=(0, dom_of(j)), device_id_type=MESH,
                ).wait_recv()

            if j == 1:
                @pl.when(g == 0)
                def _():
                    face_local().wait()

        def pair(i, _, n=n, j=j, h=h):
            for k in range(2):
                q = 2 * i + k
                at = pl.multiple_of(q * LANES, LANES)
                gather_block(send_ref, n * list_size + at, low_table if h == 0 else table, tmp.at[k])
                block = tmp[k].T[:TR]
                if h == 0:
                    face = faces_in[j, pl.ds(q, 1), :]
                    block = functools.reduce(
                        lambda x, y: x + y,
                        [jnp.where(face == float(f), block[f * LOW : (f + 1) * LOW], 0.0) for f in range(FACES)],
                    )
                    sbuf[n, 0:LOW, pl.ds(at, LANES)] = block
                else:
                    sbuf[n, :, pl.ds(at, LANES)] = block
            return 0

        lax.fori_loop(0, blocks // 2, pair, 0)
        if before is not None:
            for_send(*before, lambda copy: copy.start(), lambda copy: copy.start())
        before = (j, h)
    for_send(*before, lambda copy: copy.start(), lambda copy: copy.start())

    @pl.when(g == 0)
    def _():
        for j in RELAYED:
            relay_in(j).wait_recv()
            relay_out(j).start()

    def volume_step(b, _):
        block = bucket.at[b]
        pieces = split(block[...])
        geo_ref[b] = block[0:GROWS, :]
        derivs[...] = dot3((dx_h[...], dx_l[...]), pieces, ((1,), (0,)))
        for c in range(COMPS):
            q1, x1, q2, x2 = CURL[c]
            total = None
            for a in range(3):
                for q, x, sign in ((q1, x1, 1), (q2, x2, -1)):
                    m = block[METRIC + 3 * a + x : METRIC + 3 * a + x + 1, :]
                    at = (a * COMPS + q) * DP
                    term = m * derivs[at : at + DP, :]
                    total = term if total is None else (total + term if sign > 0 else total - term)
            vol_ref[b, c * DP : (c + 1) * DP, :] = total
        for f in range(FACES):
            w = tuple(x[f * TR : (f + 1) * TR, :] for x in (tr_h, tr_l))
            own_ref[b, f] = dot3(w, pieces, ((1,), (0,)))
        return 0

    lax.fori_loop(0, groups, volume_step, 0)

    lists = 3 * groups
    far_ref[lists * list_size : lists * list_size + 8, :] = jnp.zeros((8, LANES), F32)
    fill = jnp.zeros((LANES - TR, LANES), F32)

    @pl.when(g != 0)
    def _():
        weight_copy(1, 1).wait_recv()

    def put(l, q, block):
        far_ref[l * list_size + q * LANES : l * list_size + (q + 1) * LANES, :] = jnp.concatenate([block, fill], 0).T

    def got(j, s, rows):
        l = j * groups + s
        return pltpu.make_async_remote_copy(
            src_ref=sbuf.at[l, pl.ds(0, rows)], dst_ref=arrived.at[l, pl.ds(0, rows)], send_sem=ssem.at[l],
            recv_sem=rsem.at[l], device_id=(s, dom_of(j)), device_id_type=MESH,
        )

    for j, s in [(j, s) for j in (2, 0, 1) for s in (0, 1, 2, 3)]:
        l = j * groups + s
        first = g == 0
        rest = g != 0
        if j == 1:
            @pl.when(g == s)
            def _(s=s):
                local_copy(s, LOW if s == 0 else TR).wait()

            first = jnp.logical_and(first, g != s)
            rest = jnp.logical_and(rest, g != s)

        @pl.when(first)
        def _(j=j, s=s):
            got(j, s, LOW).wait_recv()

        @pl.when(rest)
        def _(j=j, s=s):
            got(j, s, CODED if s == 0 else TR).wait_recv()

        @pl.when(g == 0)
        def _(l=l):
            gap = jnp.zeros((PP - N1, LANES), F32)
            for q in range(blocks):
                x = arrived[l, 0:LOW, q * LANES : (q + 1) * LANES]
                parts = []
                for c in range(COMPS):
                    parts += [x[c * N1 : (c + 1) * N1], gap]
                put(l, q, jnp.concatenate(parts, 0))

        @pl.when(g != 0)
        def _(l=l, s=s):
            for q in range(blocks):
                if s == 0:
                    x = arrived[l, 0:CODED, q * LANES : (q + 1) * LANES]
                    spread = dot3(split(t1x[...]), split(x), ((0,), (0,)))
                    face = x[LOW : LOW + 1, :]
                    put(l, q, functools.reduce(
                        lambda u, v: u + v,
                        [jnp.where(face == float(f), spread[f * LANES : f * LANES + TR], 0.0) for f in range(FACES)],
                    ))
                else:
                    put(l, q, arrived[l, :, q * LANES : (q + 1) * LANES])

    for i in range(groups - 1):
        for_goal(i, lambda copy: copy.wait_send())
    for j, h in order:
        for_send(j, h, lambda copy: copy.wait_send(), lambda copy: None)

    @pl.when(g == 0)
    def _():
        for j in RELAYED:
            relay_out(j).wait_send()
        for kind in range(2):
            for h in range(1, groups):
                weight_copy(kind, h).wait_send()
        for s in range(groups):
            for j in range(3):
                if (s, j) != (0, 1):
                    face_copy(s, j).wait_send()


def cross_of(u, v):
    return [u[1] * v[2] - u[2] * v[1], u[2] * v[0] - u[0] * v[2], u[0] * v[1] - u[1] * v[0]]


def final_kernel(groups, cap, recv_ref, table, own_ref, vol_ref, geo_ref, lift_ref, out_ref, tmp, far, flux):
    slots = groups * cap
    lift = split(lift_ref[...])

    for g in range(groups):

        def one_face(f, _):
            for q in range(cap // LANES):
                gather_block(recv_ref, f * slots + g * cap + q * LANES, table, tmp.at[q % 2])
                far[f, :, q * LANES : (q + 1) * LANES] = tmp[q % 2].T[:TR]
            return 0

        lax.fori_loop(0, FACES, one_face, 0)
        for f in range(FACES):
            jump = far[f] - own_ref[g, f]
            jumps = [jump[c * PP : (c + 1) * PP, :] for c in range(COMPS)]
            n = [geo_ref[g, NORMAL + c * FACES + f : NORMAL + c * FACES + f + 1, :] for c in range(3)]
            s = 0.5 * geo_ref[g, SCALE + f : SCALE + f + 1, :]
            je, jh = jumps[:3], jumps[3:]
            ne = n[0] * je[0] + n[1] * je[1] + n[2] * je[2]
            nh = n[0] * jh[0] + n[1] * jh[1] + n[2] * jh[2]
            th, te = cross_of(n, jh), cross_of(n, je)
            for c in range(3):
                flux[c, f * PP : (f + 1) * PP, :] = s * (th[c] + je[c] - n[c] * ne)
                flux[3 + c, f * PP : (f + 1) * PP, :] = s * (jh[c] - te[c] - n[c] * nh)
        for c in range(COMPS):
            result = dot3(lift, split(flux[c]), ((1,), (0,))) + vol_ref[g, c * DP : (c + 1) * DP, :]
            out_ref[c * NPM : (c + 1) * NPM, g * cap : (g + 1) * cap] = result[:NPM]


def local(groups, doms, fields, metric, normals, fscale, orders, slots, send_faces, recv_faces, dmat, tmat, lmat):
    elements = fields.shape[1]
    cap = elements // 2
    total = groups * cap
    lists = 3 * groups
    list_size = send_faces.shape[0] // lists
    blocks = list_size // LANES
    dma = pltpu.SemaphoreType.DMA
    received, own, vol, geo, lift = pl.pallas_call(
        functools.partial(move_kernel, groups, doms, cap, list_size),
        out_shape=(
            jax.ShapeDtypeStruct((lists * list_size + 8, LANES), F32),
            jax.ShapeDtypeStruct((groups, FACES, TR, cap), F32),
            jax.ShapeDtypeStruct((groups, COMPS * DP, cap), F32),
            jax.ShapeDtypeStruct((groups, GROWS, cap), F32),
            jax.ShapeDtypeStruct((DP, FACES * PP), F32),
        ),
        in_specs=[SM] + [VM] * 10,
        out_specs=(VM,) * 5,
        scratch_shapes=[
            pltpu.VMEM((ROWS, elements), F32),
            pltpu.VMEM((groups - 1, ROWS, cap), F32),
            pltpu.VMEM((groups, ROWS, cap), F32),
            pltpu.VMEM((FACES * total + 8, LANES), F32),
            pltpu.VMEM((FACES * total + 8, LANES), F32),
            pltpu.VMEM((2, LANES, LANES), F32),
            pltpu.VMEM((lists, TR, list_size), F32),
            pltpu.VMEM((lists, TR, list_size), F32),
            pltpu.VMEM((len(RELAYED), TR, list_size), F32),
            pltpu.VMEM((5, LANES, LANES), F32),
            pltpu.VMEM((2 * FACES * LANES, ROWS), BF16),
            pltpu.VMEM((2 * FACES * LANES, ROWS), BF16),
            pltpu.VMEM((FACES * TR, ROWS), BF16),
            pltpu.VMEM((FACES * TR, ROWS), BF16),
            pltpu.VMEM((3 * COMPS * DP, ROWS), BF16),
            pltpu.VMEM((3 * COMPS * DP, ROWS), BF16),
            pltpu.VMEM((3 * COMPS * DP, cap), F32),
            pltpu.VMEM((FACES * LOW, LANES), F32),
            pltpu.VMEM((CODED, FACES * LANES), F32),
            pltpu.VMEM((lists, 8, LANES), F32),
            pltpu.VMEM((3, 8, LANES), F32),
            dma((groups - 1,)),
            dma((groups,)),
            dma((lists,)),
            dma((lists,)),
            dma((len(RELAYED),)),
            dma((len(RELAYED),)),
            dma((groups,)),
            dma((1,)),
            dma((groups,)),
            dma((1,)),
            dma((lists,)),
            dma((3,)),
        ],
        compiler_params=pltpu.CompilerParams(
            vmem_limit_bytes=40 * 1024 * 1024, collective_id=0, has_side_effects=True
        ),
        name="move",
    )(
        send_faces,
        orders.reshape(-1, LANES),
        slots.reshape(-1, LANES),
        fields,
        metric,
        normals,
        fscale,
        recv_faces.reshape(-1, LANES),
        dmat[0],
        tmat[0],
        lmat[0],
    )
    return pl.pallas_call(
        functools.partial(final_kernel, groups, cap),
        out_shape=jax.ShapeDtypeStruct((COMPS * NPM, total), F32),
        in_specs=[SM, VM, VM, VM, VM, VM],
        out_specs=VM,
        scratch_shapes=[
            pltpu.VMEM((2, LANES, LANES), F32),
            pltpu.VMEM((FACES, TR, cap), F32),
            pltpu.VMEM((COMPS, FACES * PP, cap), F32),
        ],
        compiler_params=pltpu.CompilerParams(vmem_limit_bytes=24 * 1024 * 1024),
        name="final",
    )(recv_faces, received, own, vol, geo, lift)


def solution(mesh):
    col = P(None, ("grp", "dom"))
    row = P(("grp", "dom"))
    mat = P("grp", None, None)
    in_specs = (col, col, col, col, row, row, row, row, mat, mat, mat)
    body = functools.partial(local, mesh.shape["grp"], mesh.shape["dom"])
    return jax.shard_map(body, mesh=mesh, in_specs=in_specs, out_specs=col, check_vma=False)
```

time: 99.8 us -> 92.4 us (0.926); the launches traced: 98 us -> 91.7 us
  Pallas kernels: 93.5 us -> 82.9 us
  local copies, waits for them, and re-layouts: 2.56 us -> 8.83 us
  other arithmetic: 1.77 us -> 0 us
    unnamed x23 -> x19, local copies, waits for them, and re-layouts: 2.21 us -> 8.83 us
    pallas_call x2 -> x1, Pallas kernels: 75.2 us -> 68.7 us  [local(): pl.pallas_call(functools.partial(move_kernel, groups, doms, cap, list_siz...]
    pallas_call x1, Pallas kernels: 18.3 us -> 14.2 us  [local(): pl.pallas_call(functools.partial(final_kernel, groups, cap), out_shape=ja...]
where the time goes in v1:
time: 92.4 us; the launch traced here: 91.7 us
  Pallas kernels  82.9 us (90%)
  local copies, waits for them, and re-layouts  8.83 us (10%)
    pallas_call x1, Pallas kernels, local(): pl.pallas_call(functools.partial(move_kernel, groups, doms, cap, list_siz...  68.7 us
    pallas_call x1, Pallas kernels, local(): pl.pallas_call(functools.partial(final_kernel, groups, cap), out_shape=ja...  14.2 us
    unnamed x19, local copies, waits for them, and re-layouts  8.83 us

profile of v1, /device:TPU:0, one launch (start us, length us, event | category | flops | bytes accessed | tf_op | source)
XLA Modules:
  0.0 91.7 jit_solution(6849309606175080128)
XLA Ops:
  0.0 0.7 copy.16
  0.7 0.8 copy.13
  1.5 0.8 copy.12
  2.4 0.0 copy-start
  2.4 1.2 %copy-done = f32[210,1024]{1,0:T(8,128)S(1)} copy-done((f32[210,1024]{1,0:T(8,128)S(1)}, f32[210,1024]{1,0:T(8,128)}, u32[]{:S(2)}) %copy-start) | copy-done | bytes 860184
  3.5 0.0 copy-start.1
  3.5 0.8 copy-done.1
  4.3 0.0 copy-start.2
  4.3 0.8 copy-done.2
  5.1 0.0 copy-start.3
  5.1 0.8 copy-done.3
  6.0 0.0 copy-start.4
  6.0 0.8 copy-done.4
  6.7 0.0 copy-start.5
  6.7 0.7 copy-done.5
  7.5 0.0 copy-start.6
  7.5 0.7 copy-done.6
  8.2 0.0 copy-start.7
  8.2 0.7 copy-done.7
  8.8 68.7 %move.1 = (f32[9224,128]{1,0:T(8,128)S(1)}, f32[4,4,96,512]{3,2,1,0:T(8,128)S(1)}, f32[4,240,512]{2,1,0:T(8,128)S(1)}, f32[4,32,512]{2,1,0:T(8,128)S(1)}, f32[40,64]{1,0:T(8,128)S(1)}) custom-call(s32[9216]{0:T(1024)S(1)} %copy-done.4, s32[8,128]{1,0:T(8,128)S(1)} %bitcast.12, s32[8,128]{1,0:T(8,128)S(1)} %bitcast.13, f32[210,1024]{1,0:T(8,128)S(1)} %copy-done, ...), custom_call_target="tpu_custom_call" | custom-call | tf_op jit(solution)/shard_map/move/pallas_call | solution.py:566
  77.5 14.2 %final.1 = f32[210,2048]{1,0:T(8,128)} custom-call(s32[8192]{0:T(1024)S(1)} %copy-done.1, f32[9224,128]{1,0:T(8,128)S(1)} %get-tuple-element.10.table, f32[4,4,96,512]{3,2,1,0:T(8,128)S(1)} %get-tuple-element.11.own_ref, f32[4,240,512]{2,1,0:T(8,128)S(1)} %get-tuple-element.12.vol_ref, f32[4,32,512]{2,1,0:T(8,128)S(1)} %get-tuple-element.13.geo_ref, ...), custom_call_target="tpu_custom_call" | custom-call | tf_op jit(solution)/shard_map/final/pallas_call | solution.py:629
Async XLA Ops:
  2.4 1.2 %copy-start = (f32[210,1024]{1,0:T(8,128)S(1)}, f32[210,1024]{1,0:T(8,128)}, u32[]{:S(2)}) copy-start(f32[210,1024]{1,0:T(8,128)} %fields_ref.1) | copy-start | bytes 2580484
  3.5 0.8 copy-start.1
  4.3 0.8 copy-start.2
  5.1 0.8 copy-start.3
  6.0 0.8 copy-start.4
  6.7 0.7 copy-start.5
  7.5 0.7 copy-start.6
  8.2 0.7 copy-start.7

commit v2 on v1

v2 whole, which is shorter than its diff:
```python
import functools

import jax
import jax.numpy as jnp
from jax import lax
from jax.experimental import pallas as pl
from jax.experimental.pallas import tpu as pltpu
from jax.sharding import PartitionSpec as P

NPM = 35
FPTS = 15
COMPS = 6
FACES = 4
PP = 16
DP = 40
LANES = 128
TR = COMPS * PP
NODES = (4, 10, 20, 35)
STARTS = (0, 4, 10, 20)
N1 = NODES[0]
LOW = COMPS * N1
CODED = (32, 64)
SHARE = 72
TOGETHER = 4
METRIC, NORMAL, SCALE, ONE, GEO = 0, 9, 21, 25, 26
GROWS = 32
ROWS = 240
SENT = tuple(-(-(GEO + COMPS * n) // 8) * 8 for n in NODES)
BASES = tuple(GEO + COMPS * s for s in STARTS)
RELAYED = (2, 0)
MESH = pl.DeviceIdType.MESH
F32 = jnp.float32
BF16 = jnp.bfloat16
EXACT = lax.Precision.HIGHEST


def split(x):
    high = x.astype(BF16)
    low = (x - high.astype(F32)).astype(BF16)
    return high, low


def dot3(a, b, dims):
    ah, al = a
    bh, bl = b

    def mul(x, y):
        return lax.dot_general(x, y, (dims, ((), ())), preferred_element_type=F32)

    return mul(ah, bh) + (mul(ah, bl) + mul(al, bh))


def exact_dot(a, b, dims=((1,), (0,))):
    return lax.dot_general(a, b, (dims, ((), ())), precision=EXACT, preferred_element_type=F32)


def iotas(shape):
    return lax.broadcasted_iota(jnp.int32, shape, 0), lax.broadcasted_iota(jnp.int32, shape, 1)


def ones_where(cond):
    return jnp.where(cond, 1.0, 0.0).astype(F32)


VM = pl.BlockSpec(memory_space=pltpu.VMEM)
HB = pl.BlockSpec(memory_space=pltpu.HBM)


def gather_block(index_ref, q, table, tmp):
    for i in range(LANES):
        tmp[i : i + 1, :] = table[pl.ds(index_ref[q, i], 1), :]


def flat_row(block):
    return jnp.concatenate([block[i : i + 1, :] for i in range(block.shape[0])], axis=1)


CURL = ((5, 1, 4, 2), (3, 2, 5, 0), (4, 0, 3, 1), (1, 2, 2, 1), (2, 0, 0, 2), (0, 1, 1, 0))


def place(c, shape):
    i, r = iotas(shape)
    target = BASES[3] + c * (NODES[3] - STARTS[3]) + (i - STARTS[3])
    for b in (2, 1, 0):
        width = NODES[b] - STARTS[b]
        target = jnp.where(i < NODES[b], BASES[b] + c * width + (i - STARTS[b]), target)
    return i, r, target


def coded_rows(s, shape, dim):
    i = lax.broadcasted_iota(jnp.int32, shape, dim)
    comp, node = i // N1, i & (N1 - 1)
    if s:
        width = NODES[1] - NODES[0]
        k = i - LOW
        late = (k * 43) // 256
        comp = jnp.where(i < LOW, comp, late)
        node = jnp.where(i < LOW, node, NODES[0] + k - late * width)
    return comp, node, i < COMPS * NODES[s]


def move_kernel(
    groups, doms, cap, list_size,
    send_hbm, orders_hbm, slots_hbm, fields_hbm, metric_hbm, normals_hbm, fscale_hbm, recv_hbm, dmat_hbm, tmat_hbm, lmat_hbm,
    far_ref, own_ref, vol_ref, geo_ref, lift_ref, recv_ref,
    orders_ref, slots_ref, fields_ref, metric_ref, normals_ref, fscale_ref, dmat_ref, tmat_ref, lmat_ref, send_ref, index, in_sem, index_sem,
    pay, bsend, bucket, brelay, table, low_table, tmp, sbuf, arrived, relay, wide, wcat_h, wcat_l, tr_h, tr_l, dx_h, dx_l,
    tx_h, tx_l, derivs, l1x, lift_out, lift_in, trace_out, trace_in, faces_out, faces_in,
    bsend_sem, brecv_sem, hop_sem, ssem, rsem, relay_send, relay_recv, l_send, l_recv, t_send, t_recv, fsend_sem, frecv_sem,
):
    g = lax.axis_index("grp")
    p = lax.axis_index("dom")
    slots = groups * cap
    blocks = list_size // LANES
    pairs = blocks // 2
    elements = 2 * cap
    barrier = pltpu.get_barrier_semaphore()
    loads = [
        pltpu.make_async_copy(src, dst, in_sem.at[k])
        for k, (src, dst) in enumerate(
            (
                (fields_hbm, fields_ref), (orders_hbm, orders_ref), (slots_hbm, slots_ref), (metric_hbm, metric_ref),
                (normals_hbm, normals_ref), (fscale_hbm, fscale_ref), (tmat_hbm, tmat_ref), (lmat_hbm, lmat_ref),
                (dmat_hbm, dmat_ref), (recv_hbm, recv_ref), (send_hbm, send_ref),
            )
        )
    ]
    for load in loads:
        load.start()

    def dom_of(j):
        return lax.rem(p + j - 1 + doms, doms)

    for b in range(groups):
        bucket[b, SENT[0] : ROWS, :] = jnp.zeros((ROWS - SENT[0], cap), F32)
    for j in (1, 2, 0):
        for d in range(groups):
            if (j, d) != (1, 0):
                pl.semaphore_signal(
                    barrier, inc=1, device_id=(lax.rem(g + d, groups), dom_of(j)), device_id_type=MESH
                )

    wide[...] = jnp.zeros_like(wide)
    pay[ONE : ONE + 1, :] = jnp.ones((1, elements), F32)
    pay[GEO + COMPS * NPM : ROWS, :] = jnp.zeros((ROWS - GEO - COMPS * NPM, elements), F32)
    for load in loads[:6]:
        load.wait()
    pay[METRIC : METRIC + 9, :] = metric_ref[...]
    pay[NORMAL : NORMAL + 12, :] = normals_ref[...]
    pay[SCALE : SCALE + 4, :] = fscale_ref[...]
    for b in range(4):
        width = NODES[b] - STARTS[b]
        for c in range(COMPS):
            at = BASES[b] + c * width
            pay[at : at + width, :] = fields_ref[c * NPM + STARTS[b] : c * NPM + NODES[b], :]
    target = flat_row((orders_ref[...] - 1) * cap + slots_ref[...])
    high, low = split(pay[...])
    both = jnp.concatenate([high, low], axis=0)
    step = min(cap, 256)

    def build(h, dst):
        for k in range(0, cap, step):
            ids = lax.broadcasted_iota(jnp.int32, (step, elements), 0) + (h * cap + k)
            hot = jnp.where(ids == target, 1.0, 0.0).astype(BF16)
            out = lax.dot_general(both, hot, (((1,), (1,)), ((), ())), preferred_element_type=F32)
            dst[:, k : k + step] = out[:ROWS] + out[ROWS:]

    def goal(i):
        top = groups - 1 - i
        return top - jnp.where(top <= g, 1, 0)

    def bucket_copy(i, rows):
        return pltpu.make_async_remote_copy(
            src_ref=bsend.at[i, pl.ds(0, rows)],
            dst_ref=bucket.at[g, pl.ds(0, rows)],
            send_sem=bsend_sem.at[i],
            recv_sem=brecv_sem.at[g],
            device_id=(goal(i), p),
            device_id_type=MESH,
        )

    main = ROWS - SHARE

    def hop_in():
        return pltpu.make_async_remote_copy(
            src_ref=bsend.at[0, pl.ds(main, SHARE)], dst_ref=brelay, send_sem=hop_sem.at[0], recv_sem=hop_sem.at[1],
            device_id=(2, p), device_id_type=MESH,
        )

    def hop_out():
        return pltpu.make_async_remote_copy(
            src_ref=brelay, dst_ref=bucket.at[0, pl.ds(main, SHARE)], send_sem=hop_sem.at[2], recv_sem=hop_sem.at[3],
            device_id=(3, p), device_id_type=MESH,
        )

    def for_goal(i, act):
        for h in (groups - 1 - i, groups - 2 - i):
            hit = goal(i) == h
            if i == 0 and h == groups - 1:
                @pl.when(g == 0)
                def _():
                    act(hop_in())
                    act(bucket_copy(0, main))

                hit = jnp.logical_and(hit, g != 0)

            @pl.when(hit)
            def _(h=h):
                act(bucket_copy(i, SENT[h]))

    build(goal(0), bsend.at[0])
    pl.semaphore_wait(barrier, 3 * groups - 1)
    for i in range(1, groups - 1):
        build(goal(i), bsend.at[i])
        for_goal(i - 1, lambda copy: copy.start())
    build(g, bucket.at[g])
    for_goal(groups - 2, lambda copy: copy.start())

    for load in loads[6:]:
        load.wait()

    def fetch(n, q):
        return pltpu.make_async_copy(send_ref.at[n * pairs + q], index.at[q], index_sem.at[q])

    own_nodes = (g + 2) * (g + 3) * (g + 4) // 6
    wide[0, 0:NPM, 0 : FPTS * FACES] = tmat_ref[:, 0, :]
    wide[1, 0:NPM, 0 : FPTS * FACES] = lmat_ref[:, 0, :]
    wide[2, 0:NPM, 0 : 3 * NPM] = dmat_ref[:, 0, :]
    i, r = iotas((FACES * PP, LANES))
    order_points = ones_where((r == (i & (PP - 1)) * FACES + (i // PP)) & ((i & (PP - 1)) < FPTS))
    trace = exact_dot(order_points, wide[0], ((1,), (1,)))
    lift = exact_dot(wide[1, 0:DP], order_points, ((1,), (1,)))
    row = lax.broadcasted_iota(jnp.int32, (DP, FACES * PP), 0)
    lift = jnp.where(row < own_nodes, lift, 0.0)

    def weight_copy(kind, h):
        src, dst, send, recv = (
            (lift_out, lift_in, l_send, l_recv.at[0]),
            (trace_out, trace_in.at[0], t_send, t_recv.at[0]),
            (trace_out, trace_in.at[1], t_send, t_recv.at[1]),
        )[kind]
        return pltpu.make_async_remote_copy(
            src_ref=src, dst_ref=dst, send_sem=send.at[h], recv_sem=recv, device_id=(h, p), device_id_type=MESH
        )

    trace_out[...] = trace
    lift_out[...] = jnp.zeros((8, LANES), F32)
    lift_out[:, 0 : FACES * PP] = lift[0:8]

    tr_f = [[] for _ in range(FACES)]
    node = lax.broadcasted_iota(jnp.int32, (NPM, ROWS), 0)
    for at in range(0, 3 * COMPS * DP, DP):
        dx_h[at + DP - 8 : at + DP, :] = jnp.zeros((8, ROWS), BF16)
        dx_l[at + DP - 8 : at + DP, :] = jnp.zeros((8, ROWS), BF16)
    for c in range(COMPS):
        i, r, at = place(c, (LANES, ROWS))
        spread = ones_where((r == at) & (i < own_nodes) & (i < NPM))
        part = exact_dot(trace, spread)
        for f in range(FACES):
            tr_f[f].append(part[f * PP : (f + 1) * PP])
        block = exact_dot(wide[2], spread, ((0,), (0,)))
        for a in range(3):
            piece = split(jnp.where(node < own_nodes, block[a * NPM : (a + 1) * NPM], 0.0))
            at_row = (a * COMPS + c) * DP
            dx_h[at_row : at_row + NPM, :] = piece[0]
            dx_l[at_row : at_row + NPM, :] = piece[1]
    tr_f = [jnp.concatenate(parts + [jnp.zeros((LANES - TR, ROWS), F32)], 0) for parts in tr_f]

    def face_copy(s, j):
        return pltpu.make_async_remote_copy(
            src_ref=faces_out.at[j * groups + s],
            dst_ref=faces_in.at[j],
            send_sem=fsend_sem.at[j * groups + s],
            recv_sem=frecv_sem.at[j],
            device_id=(s, lax.rem(p - j + 1 + doms, doms)),
            device_id_type=MESH,
        )

    def face_local():
        return pltpu.make_async_copy(faces_out.at[groups], faces_in.at[1], frecv_sem.at[1])

    @pl.when(g == 0)
    def _():
        lift_in[...] = lift_out[...]
        for kind in range(2):
            for h in range(1, groups):
                weight_copy(kind, h).start()
        rows = slots // LANES
        count = -(-(3 * groups * blocks) // 8) * 8
        found = jnp.zeros((count, LANES), F32)
        per = recv_ref.shape[1]
        for f in range(1, FACES):
            entry = jnp.concatenate(
                [flat_row(recv_ref[k]) for k in range(f * rows // per, (f + 1) * rows // per)], axis=1
            )
            upper, lower = entry // LANES, entry & (LANES - 1)
            a = jnp.where(lax.broadcasted_iota(jnp.int32, (count, slots), 0) == upper, float(f), 0.0).astype(BF16)
            b = jnp.where(lax.broadcasted_iota(jnp.int32, (LANES, slots), 0) == lower, 1.0, 0.0).astype(BF16)
            found = found + lax.dot_general(a, b, (((1,), (1,)), ((), ())), preferred_element_type=F32)
        for n in range(3 * groups):
            faces_out[n, 0:blocks, :] = found[n * blocks : (n + 1) * blocks]
        for s in range(groups):
            for j in range(3):
                (face_local() if (s, j) == (0, 1) else face_copy(s, j)).start()

    @pl.when(g == 1)
    def _():
        trace_in[1] = trace_out[...]
        for h in range(2, groups):
            weight_copy(2, h).start()

    @pl.when(g != 0)
    def _():
        weight_copy(0, 1).wait_recv()

    i, r = iotas((LOW, 8))
    picked = exact_dot(ones_where(r == (i & (N1 - 1))), lift_in[...])
    for f in range(FACES):
        i, r = iotas((LANES, LANES))
        fan = ones_where(i == f * PP + (r & (PP - 1)))
        i, r = iotas((LOW, LANES))
        l1x[f * LOW : (f + 1) * LOW, :] = jnp.where((r // PP) == (i // N1), exact_dot(picked, fan), 0.0)

    for f in range(FACES):
        at = f * 2 * LANES
        for k, piece in enumerate(split(tr_f[f])):
            (tr_h, tr_l)[k][f * TR : (f + 1) * TR, :] = piece[:TR]
            (wcat_h, wcat_l)[k][at : at + LANES, :] = piece
        lowered = exact_dot(l1x[...], tr_f[f])
        filled = jnp.concatenate([lowered, jnp.zeros((LANES - TR, ROWS), F32)], 0)
        for k, piece in enumerate(split(filled)):
            (wcat_h, wcat_l)[k][at + LANES : at + 2 * LANES, :] = piece

        @pl.when(g < 2)
        def _(f=f, at=at):
            used = COMPS * own_nodes
            i, r = iotas((LANES, ROWS))
            coded = jnp.where((i < used) & (r == GEO + i), 1.0, 0.0) + jnp.where((i == used) & (r == ONE), float(f), 0.0)
            wcat_h[at : at + LANES, :] = coded.astype(BF16)
            wcat_l[at : at + LANES, :] = jnp.zeros((LANES, ROWS), BF16)

        @pl.when(g == 0)
        def _(f=f, lowered=lowered):
            i, r = iotas((TR, TR))
            pick = ones_where(((i & (PP - 1)) < N1) & (r == f * LOW + (i // PP) * N1 + (i & (PP - 1))))
            for k, piece in enumerate(split(exact_dot(pick, lowered))):
                (tr_h, tr_l)[k][f * TR : (f + 1) * TR, :] = piece

    i, r = iotas((DP, FACES * PP))
    unit = ones_where((i < N1) & ((r & (PP - 1)) == i))
    lift_ref[...] = jnp.zeros_like(lift_ref)
    for c in range(TOGETHER):
        lift_ref[c * DP : (c + 1) * DP, c * FACES * PP : (c + 1) * FACES * PP] = jnp.where(g == 0, unit, lift)

    for t in (table, low_table):
        t[FACES * slots : FACES * slots + 8, :] = jnp.zeros((8, LANES), F32)

    def make_tables(b):
        coefs = split(bucket[b].T)
        for f in range(FACES):
            w = tuple(x[f * 2 * LANES : (f + 1) * 2 * LANES, :] for x in (wcat_h, wcat_l))
            rows = dot3(coefs, w, ((1,), (1,)))
            at = pl.multiple_of(f * slots + b * cap, LANES)
            table[pl.ds(at, cap), :] = rows[:, :LANES]
            low_table[pl.ds(at, cap), :] = rows[:, LANES:]

    def arrival(b, rows):
        return pltpu.make_async_remote_copy(
            src_ref=bsend.at[0, pl.ds(0, rows)], dst_ref=bucket.at[b, pl.ds(0, rows)], send_sem=bsend_sem.at[0],
            recv_sem=brecv_sem.at[b], device_id=(b, p), device_id_type=MESH,
        )

    def arrive(b):
        for h in range(groups):
            hit = g == h
            if h == groups - 1:
                @pl.when(jnp.logical_and(hit, b == 0))
                def _():
                    arrival(b, main).wait_recv()
                    hop_out().wait_recv()

                hit = jnp.logical_and(hit, b != 0)

            @pl.when(hit)
            def _(h=h):
                arrival(b, SENT[h]).wait_recv()

    @pl.when(g == 2)
    def _():
        hop_in().wait_recv()
        hop_out().start()

    def table_step(k, _):
        b = lax.rem(g - k + groups, groups)

        @pl.when(k > 0)
        def _():
            arrive(b)

        make_tables(b)
        return 0

    lax.fori_loop(0, groups, table_step, 0)

    def list_copy(j, h, rows):
        n = j * groups + h
        return pltpu.make_async_remote_copy(
            src_ref=sbuf.at[n, pl.ds(0, rows)], dst_ref=arrived.at[j * groups + g, pl.ds(0, rows)], send_sem=ssem.at[n],
            recv_sem=rsem.at[j * groups + g], device_id=(h, dom_of(j)), device_id_type=MESH,
        )

    def local_copy(h, rows):
        n = groups + h
        return pltpu.make_async_copy(sbuf.at[n, pl.ds(0, rows)], arrived.at[n, pl.ds(0, rows)], rsem.at[n])

    def relay_in(k):
        j = RELAYED[k]
        n = j * groups + 1
        return pltpu.make_async_remote_copy(
            src_ref=sbuf.at[n], dst_ref=relay.at[k], send_sem=ssem.at[n], recv_sem=relay_recv.at[k],
            device_id=(0, p), device_id_type=MESH,
        )

    def relay_out(k):
        j = RELAYED[k]
        return pltpu.make_async_remote_copy(
            src_ref=relay.at[k], dst_ref=arrived.at[j * groups + 2], send_sem=relay_send.at[k],
            recv_sem=rsem.at[j * groups + 2], device_id=(1, dom_of(j)), device_id_type=MESH,
        )

    def width_cases():
        return ((g == 0, CODED[0]), (g == 1, CODED[1]), (g >= 2, TR))

    def for_list(j, h, act, act_local):
        here = jnp.logical_and(j == 1, h == g)
        hop = jnp.logical_and(jnp.logical_and(g == 2, h == 1), j != 1)
        plain = jnp.logical_not(jnp.logical_or(here, hop))
        for hit, rows in width_cases():
            @pl.when(jnp.logical_and(hit, plain))
            def _(rows=rows):
                act(list_copy(j, h, rows))

            @pl.when(jnp.logical_and(hit, here))
            def _(rows=rows):
                act_local(local_copy(h, rows))
        for k in range(len(RELAYED)):
            @pl.when(jnp.logical_and(hop, j == RELAYED[k]))
            def _(k=k):
                act(relay_in(k))

    def for_low(j, act, act_local):
        here = jnp.logical_and(j == 1, g == 0)

        @pl.when(jnp.logical_not(here))
        def _():
            act(list_copy(j, 0, LOW))

        @pl.when(here)
        def _():
            act_local(local_copy(0, LOW))

    def turn(k):
        return jnp.where(k == 0, 2, k - 1)

    def which(k):
        pos = lax.rem(k, 3)
        first = 3 - jnp.where(g == 3, 1, jnp.where(g == 2, 2, 0))
        second = jnp.where(g == 3, 1, jnp.where(g == 2, 3, 2))
        third = jnp.maximum(g, 1)
        return turn(k // 3), jnp.where(pos == 0, first, jnp.where(pos == 1, second, third))

    def start(copy):
        copy.start()

    many = 3 * (groups - 1)

    def numbers(k):
        j, h = which(jnp.minimum(k, many - 1))
        return jnp.where(k < many, j * groups + h, turn(jnp.maximum(k - many, 0)) * groups)

    for q in range(pairs):
        fetch(numbers(0), q).start()

    def one_list(k, _):
        j, h = which(k)
        n = j * groups + h
        ahead = numbers(k + 1)
        for q in range(blocks):
            if q % 2 == 0:
                fetch(n, q // 2).wait()
            gather_block(index.at[q // 2], q % 2, table, tmp.at[q % 2])
            if q % 2:
                fetch(ahead, q // 2).start()
            sbuf[n, :, q * LANES : (q + 1) * LANES] = tmp[q % 2].T[:TR]
            if q == 1:
                @pl.when(k > 0)
                def _():
                    for_list(*which(k - 1), start, start)
        return 0

    lax.fori_loop(0, many, one_list, 0)

    def low_list(k, _):
        j = turn(k)
        n = j * groups
        ahead = turn(k + 1) * groups

        @pl.when(jnp.logical_or(g != 0, j != 1))
        def _():
            pltpu.make_async_remote_copy(
                src_ref=faces_out.at[0], dst_ref=faces_in.at[j], send_sem=fsend_sem.at[0],
                recv_sem=frecv_sem.at[j], device_id=(0, dom_of(j)), device_id_type=MESH,
            ).wait_recv()

        @pl.when(jnp.logical_and(g == 0, j == 1))
        def _():
            face_local().wait()

        for q in range(blocks):
            if q % 2 == 0:
                fetch(n, q // 2).wait()
            gather_block(index.at[q // 2], q % 2, low_table, tmp.at[q % 2])
            if q % 2:
                @pl.when(k < 2)
                def _(q=q):
                    fetch(ahead, q // 2).start()

            block = tmp[q % 2].T[:TR]
            face = faces_in[j, q : q + 1, :]
            sbuf[n, 0:LOW, q * LANES : (q + 1) * LANES] = functools.reduce(
                lambda x, y: x + y,
                [jnp.where(face == float(f), block[f * LOW : (f + 1) * LOW], 0.0) for f in range(FACES)],
            )
            if q == 1:
                @pl.when(k == 0)
                def _():
                    for_list(*which(many - 1), start, start)

                @pl.when(k > 0)
                def _():
                    for_low(turn(k - 1), start, start)
        return 0

    lax.fori_loop(0, 3, low_list, 0)
    for_low(turn(2), start, start)

    def volume_step(b, _):
        block = bucket.at[b]
        pieces = split(block[...])
        geo_ref[b] = block[0:GROWS, :]
        derivs[...] = dot3((dx_h[...], dx_l[...]), pieces, ((1,), (0,)))
        for c in range(COMPS):
            q1, x1, q2, x2 = CURL[c]
            total = None
            for a in range(3):
                for q, x, sign in ((q1, x1, 1), (q2, x2, -1)):
                    m = block[METRIC + 3 * a + x : METRIC + 3 * a + x + 1, :]
                    at = (a * COMPS + q) * DP
                    term = m * derivs[at : at + DP, :]
                    total = term if total is None else (total + term if sign > 0 else total - term)
            vol_ref[b, c * DP : (c + 1) * DP, :] = total
        for f in range(FACES):
            w = tuple(x[f * TR : (f + 1) * TR, :] for x in (tr_h, tr_l))
            own_ref[b, f] = dot3(w, pieces, ((1,), (0,)))
        return 0

    lax.fori_loop(0, groups, volume_step, 0)

    @pl.when(g != 0)
    def _():
        weight_copy(1, 1).wait_recv()

        @pl.when(g > 1)
        def _():
            weight_copy(2, 2).wait_recv()

        for s in range(2):
            for f in range(FACES):
                i, r = iotas((TR, FACES * PP))
                fan = ones_where(r == f * PP + (i & (PP - 1)))
                _, at_node, _ = coded_rows(s, (CODED[s], LANES), 0)
                _, r = iotas((CODED[s], LANES))
                rows = exact_dot(exact_dot(fan, trace_in[s]), ones_where(r == at_node), ((1,), (1,)))
                comp, _, valid = coded_rows(s, (TR, CODED[s]), 1)
                i, _ = iotas((TR, CODED[s]))
                pieces = split(jnp.where(((i // PP) == comp) & valid, rows, 0.0))
                tx_h[s, f * TR : (f + 1) * TR, 0 : CODED[s]] = pieces[0]
                tx_l[s, f * TR : (f + 1) * TR, 0 : CODED[s]] = pieces[1]

    @pl.when(g == 0)
    def _():
        for k in range(len(RELAYED)):
            relay_in(k).wait_recv()
            relay_out(k).start()

    lists = 3 * groups
    far_ref[lists * list_size : lists * list_size + 8, :] = jnp.zeros((8, LANES), F32)
    fill = jnp.zeros((LANES - TR, LANES), F32)

    def got(l, j, s, rows):
        return pltpu.make_async_remote_copy(
            src_ref=sbuf.at[l, pl.ds(0, rows)], dst_ref=arrived.at[l, pl.ds(0, rows)], send_sem=ssem.at[l],
            recv_sem=rsem.at[l], device_id=(s, dom_of(j)), device_id_type=MESH,
        )

    def take(k, _):
        j = turn(k)
        for s in range(groups):
            l = j * groups + s
            rows = CODED[s] if s < 2 else TR
            here = jnp.logical_and(j == 1, g == s)
            away = jnp.logical_not(here)
            for hit, size in ((g == 0, LOW), (g != 0, rows)):
                @pl.when(jnp.logical_and(hit, away))
                def _(size=size, l=l, s=s):
                    got(l, j, s, size).wait_recv()

            @pl.when(here)
            def _(s=s, rows=rows):
                local_copy(s, rows if s else LOW).wait()

            def put(q, block, l=l):
                at = pl.multiple_of(l * list_size + q * LANES, LANES)
                far_ref[pl.ds(at, LANES), :] = jnp.concatenate([block, fill], 0).T

            @pl.when(g == 0)
            def _(l=l, put=put):
                gap = jnp.zeros((PP - N1, LANES), F32)
                for q in range(blocks):
                    x = arrived[l, 0:LOW, q * LANES : (q + 1) * LANES]
                    parts = []
                    for c in range(COMPS):
                        parts += [x[c * N1 : (c + 1) * N1], gap]
                    put(q, jnp.concatenate(parts, 0))

            @pl.when(g != 0)
            def _(l=l, s=s, put=put, rows=rows):
                if s > 1:
                    for q in range(blocks):
                        put(q, arrived[l, :, q * LANES : (q + 1) * LANES])
                    return
                used = COMPS * NODES[s]
                w = (tx_h[s, :, 0:rows], tx_l[s, :, 0:rows])
                for q in range(0, blocks, 2):
                    x = arrived[l, 0:rows, q * LANES : (q + 2) * LANES]
                    spread = dot3(w, split(x), ((1,), (0,)))
                    face = x[used : used + 1, :]
                    block = functools.reduce(
                        lambda u, v: u + v,
                        [jnp.where(face == float(f), spread[f * TR : (f + 1) * TR], 0.0) for f in range(FACES)],
                    )
                    put(q, block[:, :LANES])
                    put(q + 1, block[:, LANES:])
        return 0

    lax.fori_loop(0, 3, take, 0)

    def sent(copy):
        copy.wait_send()

    def nothing(copy):
        pass

    for i in range(groups - 1):
        for_goal(i, sent)

    def list_sent(k, _):
        j, h = which(k)
        here = jnp.logical_and(j == 1, h == g)
        for hit, rows in width_cases():
            @pl.when(jnp.logical_and(hit, jnp.logical_not(here)))
            def _(rows=rows):
                list_copy(j, h, rows).wait_send()
        return 0

    def low_sent(k, _):
        j = turn(k)

        @pl.when(jnp.logical_or(g != 0, j != 1))
        def _():
            list_copy(j, 0, LOW).wait_send()

        return 0

    lax.fori_loop(0, many, list_sent, 0)
    lax.fori_loop(0, 3, low_sent, 0)

    @pl.when(g == 2)
    def _():
        hop_out().wait_send()

    @pl.when(g == 1)
    def _():
        for h in range(2, groups):
            weight_copy(2, h).wait_send()

    @pl.when(g == 0)
    def _():
        for k in range(len(RELAYED)):
            relay_out(k).wait_send()
        for kind in range(2):
            for h in range(1, groups):
                weight_copy(kind, h).wait_send()
        for s in range(groups):
            for j in range(3):
                if (s, j) != (0, 1):
                    face_copy(s, j).wait_send()


def cross_of(u, v):
    return [u[1] * v[2] - u[2] * v[1], u[2] * v[0] - u[0] * v[2], u[0] * v[1] - u[1] * v[0]]


def final_kernel(
    groups, cap, recv_ref, table, own_ref, vol_ref, geo_ref, lift_ref, out_hbm,
    tmp, far, flux, out, index, index_sem, out_sem,
):
    slots = groups * cap
    blocks = cap // LANES
    lift = split(lift_ref[...])

    def fetch(g, f):
        return pltpu.make_async_copy(recv_ref.at[f * groups + g], index.at[f], index_sem.at[f])

    def leave(g):
        slot = lax.rem(g, 2)
        return pltpu.make_async_copy(
            out.at[slot], out_hbm.at[:, pl.ds(pl.multiple_of(g * cap, LANES), cap)], out_sem.at[slot]
        )

    for f in range(FACES):
        fetch(0, f).start()

    def part(g, _):
        for f in range(FACES):
            fetch(g, f).wait()
            for q in range(blocks):
                gather_block(index.at[f], q, table, tmp.at[q % 2])
                far[f, :, q * LANES : (q + 1) * LANES] = tmp[q % 2].T[:TR]

            @pl.when(g < groups - 1)
            def _(f=f):
                fetch(g + 1, f).start()

        for f in range(FACES):
            jump = far[f] - own_ref[g, f]
            jumps = [jump[c * PP : (c + 1) * PP, :] for c in range(COMPS)]
            n = [geo_ref[g, NORMAL + c * FACES + f : NORMAL + c * FACES + f + 1, :] for c in range(3)]
            s = 0.5 * geo_ref[g, SCALE + f : SCALE + f + 1, :]
            je, jh = jumps[:3], jumps[3:]
            ne = n[0] * je[0] + n[1] * je[1] + n[2] * je[2]
            nh = n[0] * jh[0] + n[1] * jh[1] + n[2] * jh[2]
            th, te = cross_of(n, jh), cross_of(n, je)
            for c in range(3):
                at = (c * FACES + f) * PP
                flux[at : at + PP, :] = s * (th[c] + je[c] - n[c] * ne)
                at += 3 * FACES * PP
                flux[at : at + PP, :] = s * (jh[c] - te[c] - n[c] * nh)

        @pl.when(g > 1)
        def _():
            leave(g - 2).wait()

        slot = lax.rem(g, 2)
        for c in range(0, COMPS, TOGETHER):
            count = min(TOGETHER, COMPS - c)
            deep = count * FACES * PP
            w = tuple(x[: count * DP, :deep] for x in lift)
            lifted = dot3(w, split(flux[c * FACES * PP : c * FACES * PP + deep, :]), ((1,), (0,)))
            lifted = lifted + vol_ref[g, c * DP : (c + count) * DP, :]
            for k in range(count):
                out[slot, (c + k) * NPM : (c + k + 1) * NPM, :] = lifted[k * DP : k * DP + NPM]
        leave(g).start()
        return 0

    lax.fori_loop(0, groups, part, 0)
    leave(groups - 2).wait()
    leave(groups - 1).wait()


def local(groups, doms, fields, metric, normals, fscale, orders, slots, send_faces, recv_faces, dmat, tmat, lmat):
    elements = fields.shape[1]
    cap = elements // 2
    total = groups * cap
    lists = 3 * groups
    list_size = send_faces.shape[0] // lists
    blocks = list_size // LANES
    dma = pltpu.SemaphoreType.DMA
    i32 = jnp.int32
    vmem = pltpu.VMEM
    recv_shape = (FACES * groups, cap // LANES, LANES)
    received, own, vol, geo, lift, entries = pl.pallas_call(
        functools.partial(move_kernel, groups, doms, cap, list_size),
        out_shape=(
            jax.ShapeDtypeStruct((lists * list_size + 8, LANES), F32),
            jax.ShapeDtypeStruct((groups, FACES, TR, cap), F32),
            jax.ShapeDtypeStruct((groups, COMPS * DP, cap), F32),
            jax.ShapeDtypeStruct((groups, GROWS, cap), F32),
            jax.ShapeDtypeStruct((TOGETHER * DP, TOGETHER * FACES * PP), F32),
            jax.ShapeDtypeStruct(recv_shape, i32),
        ),
        in_specs=[HB] * 11,
        out_specs=(VM,) * 6,
        scratch_shapes=[
            vmem((elements // LANES, LANES), i32),
            vmem((elements // LANES, LANES), i32),
            vmem(fields.shape, F32),
            vmem(metric.shape, F32),
            vmem(normals.shape, F32),
            vmem(fscale.shape, F32),
            vmem((NPM, 1, 3 * NPM), F32),
            vmem((NPM, 1, FPTS * FACES), F32),
            vmem((NPM, 1, FPTS * FACES), F32),
            vmem((lists * blocks // 2, 2, LANES), i32),
            pltpu.SMEM((blocks // 2, 2, LANES), i32),
            dma((11,)),
            dma((blocks // 2,)),
            vmem((ROWS, elements), F32),
            vmem((groups - 1, ROWS, cap), F32),
            vmem((groups, ROWS, cap), F32),
            vmem((SHARE, cap), F32),
            vmem((FACES * total + 8, LANES), F32),
            vmem((FACES * total + 8, LANES), F32),
            vmem((2, LANES, LANES), F32),
            vmem((lists, TR, list_size), F32),
            vmem((lists, TR, list_size), F32),
            vmem((len(RELAYED), TR, list_size), F32),
            vmem((3, LANES, LANES), F32),
            vmem((2 * FACES * LANES, ROWS), BF16),
            vmem((2 * FACES * LANES, ROWS), BF16),
            vmem((FACES * TR, ROWS), BF16),
            vmem((FACES * TR, ROWS), BF16),
            vmem((3 * COMPS * DP, ROWS), BF16),
            vmem((3 * COMPS * DP, ROWS), BF16),
            vmem((2, FACES * TR, LANES), BF16),
            vmem((2, FACES * TR, LANES), BF16),
            vmem((3 * COMPS * DP, cap), F32),
            vmem((FACES * LOW, LANES), F32),
            vmem((8, LANES), F32),
            vmem((8, LANES), F32),
            vmem((FACES * PP, LANES), F32),
            vmem((2, FACES * PP, LANES), F32),
            vmem((lists, 8, LANES), F32),
            vmem((3, 8, LANES), F32),
            dma((groups - 1,)),
            dma((groups,)),
            dma((4,)),
            dma((lists,)),
            dma((lists,)),
            dma((len(RELAYED),)),
            dma((len(RELAYED),)),
            dma((groups,)),
            dma((1,)),
            dma((groups,)),
            dma((2,)),
            dma((lists,)),
            dma((3,)),
        ],
        compiler_params=pltpu.CompilerParams(
            vmem_limit_bytes=40 * 1024 * 1024, collective_id=0, has_side_effects=True
        ),
        name="move",
    )(
        *[
            pltpu.with_memory_space_constraint(x, pltpu.HBM)
            for x in (
                send_faces.reshape(-1, 2, LANES),
                orders.reshape(-1, LANES),
                slots.reshape(-1, LANES),
                fields,
                metric,
                normals,
                fscale,
                recv_faces.reshape(recv_shape),
                jnp.transpose(dmat, (2, 0, 1)),
                jnp.transpose(tmat, (2, 0, 1)),
                jnp.transpose(lmat, (1, 0, 2)),
            )
        ]
    )
    return pl.pallas_call(
        functools.partial(final_kernel, groups, cap),
        out_shape=jax.ShapeDtypeStruct((COMPS * NPM, total), F32),
        in_specs=[VM] * 6,
        out_specs=HB,
        scratch_shapes=[
            vmem((2, LANES, LANES), F32),
            vmem((FACES, TR, cap), F32),
            vmem((COMPS * FACES * PP, cap), F32),
            vmem((2, COMPS * NPM, cap), F32),
            pltpu.SMEM((FACES, cap // LANES, LANES), i32),
            dma((FACES,)),
            dma((2,)),
        ],
        compiler_params=pltpu.CompilerParams(vmem_limit_bytes=24 * 1024 * 1024),
        name="final",
    )(entries, received, own, vol, geo, lift)


def solution(mesh):
    col = P(None, ("grp", "dom"))
    row = P(("grp", "dom"))
    mat = P("grp", None, None)
    in_specs = (col, col, col, col, row, row, row, row, mat, mat, mat)
    body = functools.partial(local, mesh.shape["grp"], mesh.shape["dom"])
    return jax.shard_map(body, mesh=mesh, in_specs=in_specs, out_specs=col, check_vma=False)
```

time: 92.4 us -> 79.9 us (0.86)
  the two profiles are of different devices: /device:TPU:0 before, /device:TPU:19 now
where the time goes in v2:
time: 79.9 us; the launch traced here: 79.7 us
  Pallas kernels  79.6 us (100%)
    pallas_call x1, Pallas kernels, local(): pl.pallas_call(functools.partial(move_kernel, groups, doms, cap, list_siz...  68.3 us
    pallas_call x1, Pallas kernels, local(): pl.pallas_call(functools.partial(final_kernel, groups, cap), out_shape=ja...  11.2 us

profile of v2, /device:TPU:19, one launch (start us, length us, event | category | flops | bytes accessed | tf_op | source)
XLA Modules:
  0.0 79.7 jit_solution(15840792804913886223)
XLA Ops:
  0.0 68.3 %move.1 = (f32[9224,128]{1,0:T(8,128)S(1)}, f32[4,4,96,512]{3,2,1,0:T(8,128)S(1)}, f32[4,240,512]{2,1,0:T(8,128)S(1)}, f32[4,32,512]{2,1,0:T(8,128)S(1)}, f32[16...) custom-call(s32[36,2,128]{2,1,0:T(2,128)} %bitcast.7, s32[8,128]{1,0:T(8,128)} %bitcast.12, s32[8,128]{1,0:T(8,128)} %bitcast.13, ...), custom_call_target="tpu_custom_call" | custom-call | tf_op jit(solution)/shard_map/move/pallas_call | solution.py:792
  68.3 11.2 %final.1 = f32[210,2048]{1,0:T(8,128)} custom-call(s32[16,4,128]{2,1,0:T(4,128)S(1)} %get-tuple-element.11.recv_ref, f32[9224,128]{1,0:T(8,128)S(1)} %get-tuple-element.12.table, f32[4,4,96,512]{3,2,1,0:T(8,128)S(1)} %get-tuple-element.13.own_ref, f32[4,240,512]{2,1,0:T(8,128)S(1)} %get-tuple-element.14.vol_ref, ...), custom_call_target="tpu_custom_call" | custom-call | tf_op jit(solution)/shard_map/final/pallas_call | solution.py:881

commit v3 on v2

--- a/solution.py
+++ b/solution.py
@@ -103,7 +103,7 @@
     groups, doms, cap, list_size,
     send_hbm, orders_hbm, slots_hbm, fields_hbm, metric_hbm, normals_hbm, fscale_hbm, recv_hbm, dmat_hbm, tmat_hbm, lmat_hbm,
     far_ref, own_ref, vol_ref, geo_ref, lift_ref, recv_ref,
-    orders_ref, slots_ref, fields_ref, metric_ref, normals_ref, fscale_ref, dmat_ref, tmat_ref, lmat_ref, send_ref, index, in_sem, index_sem,
+    orders_ref, slots_ref, fields_ref, metric_ref, normals_ref, fscale_ref, dmat_ref, tmat_ref, lmat_ref, send_ref, in_sem,
     pay, bsend, bucket, brelay, table, low_table, tmp, sbuf, arrived, relay, wide, wcat_h, wcat_l, tr_h, tr_l, dx_h, dx_l,
     tx_h, tx_l, derivs, l1x, lift_out, lift_in, trace_out, trace_in, faces_out, faces_in,
     bsend_sem, brecv_sem, hop_sem, ssem, rsem, relay_send, relay_recv, l_send, l_recv, t_send, t_recv, fsend_sem, frecv_sem,
@@ -218,9 +218,6 @@
 
     for load in loads[6:]:
         load.wait()
-
-    def fetch(n, q):
-        return pltpu.make_async_copy(send_ref.at[n * pairs + q], index.at[q], index_sem.at[q])
 
     own_nodes = (g + 2) * (g + 3) * (g + 4) // 6
     wide[0, 0:NPM, 0 : FPTS * FACES] = tmat_ref[:, 0, :]
@@ -418,14 +415,14 @@
         n = j * groups + 1
         return pltpu.make_async_remote_copy(
             src_ref=sbuf.at[n], dst_ref=relay.at[k], send_sem=ssem.at[n], recv_sem=relay_recv.at[k],
-            device_id=(0, p), device_id_type=MESH,
+            device_id=(0, dom_of(j)), device_id_type=MESH,
         )
 
     def relay_out(k):
         j = RELAYED[k]
         return pltpu.make_async_remote_copy(
             src_ref=relay.at[k], dst_ref=arrived.at[j * groups + 2], send_sem=relay_send.at[k],
-            recv_sem=rsem.at[j * groups + 2], device_id=(1, dom_of(j)), device_id_type=MESH,
+            recv_sem=rsem.at[j * groups + 2], device_id=(1, p), device_id_type=MESH,
         )
 
     def width_cases():
@@ -463,34 +460,23 @@
         return jnp.where(k == 0, 2, k - 1)
 
     def which(k):
-        pos = lax.rem(k, 3)
-        first = 3 - jnp.where(g == 3, 1, jnp.where(g == 2, 2, 0))
-        second = jnp.where(g == 3, 1, jnp.where(g == 2, 3, 2))
-        third = jnp.maximum(g, 1)
-        return turn(k // 3), jnp.where(pos == 0, first, jnp.where(pos == 1, second, third))
+        pos, lap = lax.rem(k, 3), k // 3
+        first = jnp.where(g == 1, 1, jnp.where(g == 2, 1, 2))
+        second = jnp.where(g == 1, 2, jnp.where(g == 2, 3, 1))
+        third = jnp.where(g == 2, 2, 3)
+        j = jnp.where(lap == 2, 1, jnp.where(lax.rem(lap + pos, 2) == 0, 2, 0))
+        return j, jnp.where(pos == 0, first, jnp.where(pos == 1, second, third))
 
     def start(copy):
         copy.start()
 
     many = 3 * (groups - 1)
-
-    def numbers(k):
-        j, h = which(jnp.minimum(k, many - 1))
-        return jnp.where(k < many, j * groups + h, turn(jnp.maximum(k - many, 0)) * groups)
-
-    for q in range(pairs):
-        fetch(numbers(0), q).start()
 
     def one_list(k, _):
         j, h = which(k)
         n = j * groups + h
-        ahead = numbers(k + 1)
         for q in range(blocks):
-            if q % 2 == 0:
-                fetch(n, q // 2).wait()
-            gather_block(index.at[q // 2], q % 2, table, tmp.at[q % 2])
-            if q % 2:
-                fetch(ahead, q // 2).start()
+            gather_block(send_ref.at[n * pairs + q // 2], q % 2, table, tmp.at[q % 2])
             sbuf[n, :, q * LANES : (q + 1) * LANES] = tmp[q % 2].T[:TR]
             if q == 1:
                 @pl.when(k > 0)
@@ -503,7 +489,6 @@
     def low_list(k, _):
         j = turn(k)
         n = j * groups
-        ahead = turn(k + 1) * groups
 
         @pl.when(jnp.logical_or(g != 0, j != 1))
         def _():
@@ -517,14 +502,7 @@
             face_local().wait()
 
         for q in range(blocks):
-            if q % 2 == 0:
-                fetch(n, q // 2).wait()
-            gather_block(index.at[q // 2], q % 2, low_table, tmp.at[q % 2])
-            if q % 2:
-                @pl.when(k < 2)
-                def _(q=q):
-                    fetch(ahead, q // 2).start()
-
+            gather_block(send_ref.at[n * pairs + q // 2], q % 2, low_table, tmp.at[q % 2])
             block = tmp[q % 2].T[:TR]
             face = faces_in[j, q : q + 1, :]
             sbuf[n, 0:LOW, q * LANES : (q + 1) * LANES] = functools.reduce(
@@ -723,45 +701,43 @@
         return pltpu.make_async_copy(recv_ref.at[f * groups + g], index.at[f], index_sem.at[f])
 
     def leave(g):
-        slot = lax.rem(g, 2)
-        return pltpu.make_async_copy(
-            out.at[slot], out_hbm.at[:, pl.ds(pl.multiple_of(g * cap, LANES), cap)], out_sem.at[slot]
-        )
+        return pltpu.make_async_copy(out.at[g % 2], out_hbm.at[:, pl.ds(g * cap, cap)], out_sem.at[g % 2])
 
     for f in range(FACES):
         fetch(0, f).start()
 
-    def part(g, _):
+    def gather_face(g, f):
+        fetch(g, f).wait()
+        for q in range(blocks):
+            gather_block(index.at[f], q, table, tmp.at[q % 2])
+            far[g % 2, f, :, q * LANES : (q + 1) * LANES] = tmp[q % 2].T[:TR]
+        if g < groups - 1:
+            fetch(g + 1, f).start()
+
+    def flux_face(g, f):
+        jump = far[g % 2, f] - own_ref[g, f]
+        jumps = [jump[c * PP : (c + 1) * PP, :] for c in range(COMPS)]
+        n = [geo_ref[g, NORMAL + c * FACES + f : NORMAL + c * FACES + f + 1, :] for c in range(3)]
+        s = 0.5 * geo_ref[g, SCALE + f : SCALE + f + 1, :]
+        je, jh = jumps[:3], jumps[3:]
+        ne = n[0] * je[0] + n[1] * je[1] + n[2] * je[2]
+        nh = n[0] * jh[0] + n[1] * jh[1] + n[2] * jh[2]
+        th, te = cross_of(n, jh), cross_of(n, je)
+        for c in range(3):
+            at = (c * FACES + f) * PP
+            flux[at : at + PP, :] = s * (th[c] + je[c] - n[c] * ne)
+            at += 3 * FACES * PP
+            flux[at : at + PP, :] = s * (jh[c] - te[c] - n[c] * nh)
+
+    for f in range(FACES):
+        gather_face(0, f)
+    for g in range(groups):
         for f in range(FACES):
-            fetch(g, f).wait()
-            for q in range(blocks):
-                gather_block(index.at[f], q, table, tmp.at[q % 2])
-                far[f, :, q * LANES : (q + 1) * LANES] = tmp[q % 2].T[:TR]
-
-            @pl.when(g < groups - 1)
-            def _(f=f):
-                fetch(g + 1, f).start()
-
-        for f in range(FACES):
-            jump = far[f] - own_ref[g, f]
-            jumps = [jump[c * PP : (c + 1) * PP, :] for c in range(COMPS)]
-            n = [geo_ref[g, NORMAL + c * FACES + f : NORMAL + c * FACES + f + 1, :] for c in range(3)]
-            s = 0.5 * geo_ref[g, SCALE + f : SCALE + f + 1, :]
-            je, jh = jumps[:3], jumps[3:]
-            ne = n[0] * je[0] + n[1] * je[1] + n[2] * je[2]
-            nh = n[0] * jh[0] + n[1] * jh[1] + n[2] * jh[2]
-            th, te = cross_of(n, jh), cross_of(n, je)
-            for c in range(3):
-                at = (c * FACES + f) * PP
-                flux[at : at + PP, :] = s * (th[c] + je[c] - n[c] * ne)
-                at += 3 * FACES * PP
-                flux[at : at + PP, :] = s * (jh[c] - te[c] - n[c] * nh)
-
-        @pl.when(g > 1)
-        def _():
+            if g < groups - 1:
+                gather_face(g + 1, f)
+            flux_face(g, f)
+        if g > 1:
             leave(g - 2).wait()
-
-        slot = lax.rem(g, 2)
         for c in range(0, COMPS, TOGETHER):
             count = min(TOGETHER, COMPS - c)
             deep = count * FACES * PP
@@ -769,11 +745,8 @@
             lifted = dot3(w, split(flux[c * FACES * PP : c * FACES * PP + deep, :]), ((1,), (0,)))
             lifted = lifted + vol_ref[g, c * DP : (c + count) * DP, :]
             for k in range(count):
-                out[slot, (c + k) * NPM : (c + k + 1) * NPM, :] = lifted[k * DP : k * DP + NPM]
+                out[g % 2, (c + k) * NPM : (c + k + 1) * NPM, :] = lifted[k * DP : k * DP + NPM]
         leave(g).start()
-        return 0
-
-    lax.fori_loop(0, groups, part, 0)
     leave(groups - 2).wait()
     leave(groups - 1).wait()
 
@@ -811,10 +784,8 @@
             vmem((NPM, 1, 3 * NPM), F32),
             vmem((NPM, 1, FPTS * FACES), F32),
             vmem((NPM, 1, FPTS * FACES), F32),
-            vmem((lists * blocks // 2, 2, LANES), i32),
-            pltpu.SMEM((blocks // 2, 2, LANES), i32),
+            pltpu.SMEM((lists * blocks // 2, 2, LANES), i32),
             dma((11,)),
-            dma((blocks // 2,)),
             vmem((ROWS, elements), F32),
             vmem((groups - 1, ROWS, cap), F32),
             vmem((groups, ROWS, cap), F32),
@@ -885,7 +856,7 @@
         out_specs=HB,
         scratch_shapes=[
             vmem((2, LANES, LANES), F32),
-            vmem((FACES, TR, cap), F32),
+            vmem((2, FACES, TR, cap), F32),
             vmem((COMPS * FACES * PP, cap), F32),
             vmem((2, COMPS * NPM, cap), F32),
             pltpu.SMEM((FACES, cap // LANES, LANES), i32),

time: 79.9 us -> 74.4 us (0.931)
  the two profiles are of different devices: /device:TPU:19 before, /device:TPU:0 now
where the time goes in v3:
time: 74.4 us; the launch traced here: 73 us
  Pallas kernels  72.9 us (98%)
    pallas_call x1, Pallas kernels, local(): pl.pallas_call(functools.partial(move_kernel, groups, doms, cap, list_siz...  62.5 us
    pallas_call x1, Pallas kernels, local(): pl.pallas_call(functools.partial(final_kernel, groups, cap), out_shape=ja...  10.4 us

profile of v3, /device:TPU:0, one launch (start us, length us, event | category | flops | bytes accessed | tf_op | source)
XLA Modules:
  0.0 73.0 jit_solution(3296346444131683055)
XLA Ops:
  0.0 62.5 %move.1 = (f32[9224,128]{1,0:T(8,128)S(1)}, f32[4,4,96,512]{3,2,1,0:T(8,128)S(1)}, f32[4,240,512]{2,1,0:T(8,128)S(1)}, f32[4,32,512]{2,1,0:T(8,128)S(1)}, f32[16...) custom-call(s32[36,2,128]{2,1,0:T(2,128)} %bitcast.7, s32[8,128]{1,0:T(8,128)} %bitcast.12, s32[8,128]{1,0:T(8,128)} %bitcast.13, ...), custom_call_target="tpu_custom_call" | custom-call | tf_op jit(solution)/shard_map/move/pallas_call | solution.py:765
  62.5 10.4 %final.1 = f32[210,2048]{1,0:T(8,128)} custom-call(s32[16,4,128]{2,1,0:T(4,128)S(1)} %get-tuple-element.11.recv_ref, f32[9224,128]{1,0:T(8,128)S(1)} %get-tuple-element.12.table, f32[4,4,96,512]{3,2,1,0:T(8,128)S(1)} %get-tuple-element.13.own_ref, f32[4,240,512]{2,1,0:T(8,128)S(1)} %get-tuple-element.14.vol_ref, ...), custom_call_target="tpu_custom_call" | custom-call | tf_op jit(solution)/shard_map/final/pallas_call | solution.py:852
